TPU v7x, 32 devices: a whole 2x2x4 slice. The times are simulated.
32 devices in a mesh: blk: 8 (over z, y), sub: 4 (over x, core).
Axes of the slice: x: 2, y: 2, z: 4, core: 2. Of those that a mesh axis runs over, the one named last changes fastest.
Arguments:
- solution: float32 [5, 8, 32, 512], P(None, 'blk', 'sub'), may hold values from -6 to 6
- right_side: float32 [5, 8, 32, 512], P(None, 'blk', 'sub'), may hold values from -6 to 6
- couple: float32 [3, 7, 5, 5], replicated, may hold values from -0.06 to 1.1, as said below
- partner: int32 [8], replicated, may hold values from 0 to 7, each once
- orient: int32 [8], replicated, may hold values from 0 to 3
- owner_one: int32 [8], replicated, may hold values from 0 to 7, each once
- owner_two: int32 [8], replicated, may hold values from 0 to 7, each once
Outputs:
- corrected: float32 [5, 8, 32, 512], P(None, 'blk', 'sub')
- coarse_one: float32 [5, 8, 16, 128], P(None, 'blk', 'sub')
- coarse_two: float32 [5, 8, 8, 32], P(None, 'blk', 'sub')
- norms: float32 [3], replicated
Inputs may be any that keep to these rules, and one draw needn't show every extreme that they name: `couple`: each level's centre matrix has diagonal entries of 0.9 to 1.1 and off-diagonal entries of magnitude 0.06 or less; every coupling's entries lie in the stated range. `partner`: A permutation of the 8 blocks. `owner_one`: A permutation of the 8 blocks. `owner_two`: A permutation of the 8 blocks.
All inputs are finite; a program needn't handle non-finite values.
Results may differ from a plain program's by a relative error of at most 0.00025.
Values sent between devices are 32-bit elements; how exact they have to be, the bound alone decides.
A program may use at most 64 MiB of HBM per device.

v0:
```python
import functools

import jax
import jax.numpy as jnp
from jax import lax
from jax.experimental import pallas as pl
from jax.experimental.pallas import tpu as pltpu
from jax.sharding import PartitionSpec as P

BI = 32
BJ = 16
SWEEPS_FINE = 2
SWEEPS_MID = 2
SWEEPS_COARSE = 4
LANES = 128
SUBLANES = 8
NV = 5
PRECISE = lax.Precision.HIGHEST
MESH = pl.DeviceIdType.MESH

RAW = 0
INV, IM, IP, JM, JP, FWD, BWD = 7, 8, 9, 10, 11, 12, 13
F2, F4, F8, FP, B2, B4, B8, BP = 14, 15, 16, 17, 18, 19, 20, 21


def product(left, right):
    total = left[0][None] * right[:, 0][:, None]
    for b in range(1, NV):
        total = total + left[b][None] * right[:, b][:, None]
    return total


def kernel(
    sizes, solution, right_side, couple, partner, orient, owner_one, owner_two,
    corrected, out_one, out_two, norms,
    coef, coef_one, coef_two, cg, sf, yf, tf, zf, enter, plane_below, plane_above,
    xsend, xrecv_a, xrecv_b, xrecv_c, up_recv, low_recv, prefix, gathered, rsum,
    down,
    field_f, field_c, field_p, field_v, field_y,
    two_f, two_c, two_p, two_v, two_y, spread,
    xs_sem, xr_sem, hs_sem, hr_sem, ps_sem, pr_sem, gs_sem, gr_sem, es_sem, er_sem,
):
    blocks, subs = sizes
    me = lax.axis_index("blk")
    sub = lax.axis_index("sub")
    last = subs - 1
    is_low = sub == 0
    is_high = sub == last
    rows = solution.shape[1]
    planes = SUBLANES
    xrecv = (xrecv_a, xrecv_b, xrecv_c)

    def edge_copy(t, b):
        return pltpu.make_async_remote_copy(
            src_ref=xsend.at[t], dst_ref=xrecv[t].at[me], send_sem=xs_sem.at[t, b],
            recv_sem=xr_sem.at[t, me], device_id=(b, last - sub), device_id_type=MESH)

    def edge_wait(t, b):
        pltpu.make_async_remote_copy(
            src_ref=xsend.at[t], dst_ref=xrecv[t].at[b], send_sem=xs_sem.at[t, b],
            recv_sem=xr_sem.at[t, b], device_id=(b, last - sub), device_id_type=MESH).wait_recv()

    def send_edge(t, ref):
        @pl.when(is_low)
        def _():
            xsend[t] = ref[:, :, 0:1, :]

        @pl.when(is_high)
        def _():
            xsend[t] = ref[:, :, planes - 1:planes, :]

        @pl.when(is_low | is_high)
        def _():
            @pl.loop(0, blocks)
            def _(b):
                edge_copy(t, b).start()

    lane = lax.broadcasted_iota(jnp.int32, (1, LANES), 1)

    def lane_xor(x, bit):
        axis = x.ndim - 1
        mask = (lane & bit) != 0
        return jnp.where(mask, pltpu.roll(x, bit, axis), pltpu.roll(x, LANES - bit, axis))

    def receive_edge(t):
        @pl.when(is_low | is_high)
        def _():
            @pl.loop(0, blocks)
            def _(b):
                edge_wait(t, b)

        def oriented(source, code):
            got = xrecv[t][source]
            swapped = jnp.concatenate([got[:, r:r + 1] for r in range(rows - 1, -1, -1)], axis=1)
            for bit in (16, 32, 64):
                swapped = lane_xor(swapped, bit)
            got = jnp.where(code % 2 == 1, swapped, got)
            swapped = got
            for bit in (1, 2, 4, 8):
                swapped = lane_xor(swapped, bit)
            return jnp.where(code // 2 == 1, swapped, got)

        @pl.when(is_low)
        def _():
            source = down[me]
            plane_below[...] = oriented(source, orient[source])

        @pl.when(is_high)
        def _():
            plane_above[...] = oriented(partner[me], orient[me])

    def halo_copy(which, src, dst, target):
        return pltpu.make_async_remote_copy(
            src_ref=src, dst_ref=dst, send_sem=hs_sem.at[which], recv_sem=hr_sem.at[which],
            device_id=(me, target), device_id_type=MESH)

    def prefix_copy(n, source, target):
        return pltpu.make_async_remote_copy(
            src_ref=prefix.at[n, source], dst_ref=prefix.at[n, source], send_sem=ps_sem.at[n, target],
            recv_sem=pr_sem.at[n, source], device_id=(me, target), device_id_type=MESH)

    send_edge(0, solution)
    up_recv[1] = solution[:, :, 0:1, :]

    @pl.when(jnp.logical_not(is_low))
    def _():
        halo_copy(0, up_recv.at[1], up_recv.at[0], sub - 1).start()

    def found(mapping, value):
        return lax.fori_loop(0, blocks, lambda n, best: jnp.where(mapping[n] == value, n, best), 0)

    @pl.loop(0, blocks)
    def _(n):
        down[n] = found(partner, n)

    held = (found(owner_one, me), found(owner_two, me))

    def splat(level, matrix):
        base = (level * 7 + matrix) * NV * NV
        return jnp.stack([
            jnp.stack([jnp.full((SUBLANES, LANES), couple[base + a * NV + b], jnp.float32) for a in range(NV)])
            for b in range(NV)
        ])

    identity = jnp.stack([
        jnp.stack([jnp.full((SUBLANES, LANES), 1.0 if a == b else 0.0, jnp.float32) for a in range(NV)])
        for b in range(NV)
    ])

    def prepare(level, store):
        for matrix in range(7):
            store[RAW + matrix] = splat(level, matrix)
        store[INV] = identity

        @pl.loop(0, 6)
        def _(repeat):
            approx = store[INV]
            store[INV] = product(approx, 2.0 * identity - product(store[RAW], approx))

        @pl.loop(0, 6)
        def _(matrix):
            store[IM + matrix] = product(store[INV], store[RAW + 1 + matrix])

    prepare(0, coef)
    place = lax.broadcasted_iota(jnp.int32, (SUBLANES, LANES), 0)

    def powers(base, second, count):
        coef[second] = product(coef[base], coef[base])
        coef[second + 1] = product(coef[second], coef[second])
        coef[second + 2] = product(coef[second + 1], coef[second + 1])
        run = jnp.where((count & 1) != 0, coef[base], identity)
        for bit, index in ((2, second), (4, second + 1), (8, second + 2)):
            run = product(jnp.where((count & bit) != 0, coef[index], identity), run)
        coef[second + 3] = run

    powers(FWD, F2, place + 1)
    powers(BWD, B2, planes - place)

    def apply(index, values, height=SUBLANES):
        total = None
        for b in range(NV):
            term = coef[index, b][:, None, :height] * values[b][None]
            total = term if total is None else total + term
        return total

    in_low = lane < BJ
    in_high = lane >= LANES - BJ
    j_first = (lane & (BJ - 1)) == 0
    j_final = (lane & (BJ - 1)) == BJ - 1

    def lateral(values, base):
        zero = jnp.zeros_like(values[:, :1])
        turned = pltpu.roll(values, BJ, 3)
        total = apply(base, jnp.where(in_low, jnp.concatenate([zero, turned[:, :-1]], axis=1), turned))
        turned = pltpu.roll(values, LANES - BJ, 3)
        total = total + apply(base + 1, jnp.where(in_high, jnp.concatenate([turned[:, 1:], zero], axis=1), turned))
        total = total + apply(base + 2, jnp.where(j_first, 0.0, pltpu.roll(values, 1, 3)))
        return total + apply(base + 3, jnp.where(j_final, 0.0, pltpu.roll(values, LANES - 1, 3)))

    def moved_up(values, by):
        return pltpu.roll(values, by, 2)

    def scan(values, first, second, reverse):
        for by, index in ((1, first), (2, second), (4, second + 1)):
            if reverse:
                shifted = jnp.where(place < planes - by, pltpu.roll(values, planes - by, 2), 0.0)
            else:
                shifted = jnp.where(place >= by, pltpu.roll(values, by, 2), 0.0)
            values = values + apply(index, shifted)
        return values

    def complete(n, ref, boundary, reverse, index_all, index_block):
        starts = is_high if reverse else is_low

        @pl.when(starts)
        def _():
            ref[...] = ref[...] + apply(index_all, boundary[...])

        prefix[n, sub] = ref[:, :, 0:1, :] if reverse else ref[:, :, planes - 1:planes, :]
        for target in range(subs):
            @pl.when((target < sub) if reverse else (target > sub))
            def _():
                prefix_copy(n, sub, target).start()

        @pl.when(jnp.logical_not(starts))
        def _():
            enter[...] = jnp.zeros_like(enter)
            order = range(last, 0, -1) if reverse else range(last)
            for source in order:
                @pl.when((source > sub) if reverse else (source < sub))
                def _():
                    prefix_copy(n, source, sub).wait_recv()
                    enter[...] = prefix[n, source] + apply(index_block, enter[...], 1)
            ref[...] = ref[...] + apply(index_all, enter[...])

    cg[...] = apply(INV, right_side[...])
    sf[...] = cg[...] + lateral(solution[...], IM)
    for t in range(SWEEPS_FINE):
        if t > 0:
            sf[...] = cg[...] + lateral(zf[...], IM) + (zf[...] - tf[...])
        receive_edge(t)
        if t == 0:
            @pl.when(is_high)
            def _():
                up_recv[0] = plane_above[...]

            @pl.when(jnp.logical_not(is_high))
            def _():
                halo_copy(0, up_recv.at[1], up_recv.at[0], sub).wait_recv()

            upper = jnp.where(place == planes - 1, up_recv[0], pltpu.roll(solution[...], planes - 1, 2))
            sf[...] = sf[...] + apply(BWD, upper)
        else:
            @pl.when(is_high)
            def _():
                fresh = apply(BWD, plane_above[...], 1)
                old = zf[:, :, planes - 1:planes, :] - tf[:, :, planes - 1:planes, :]
                sf[:, :, planes - 1:planes, :] = sf[:, :, planes - 1:planes, :] + (fresh - old)

        yf[...] = scan(sf[...], FWD, F2, False)
        complete(2 * t, yf, plane_below, False, FP, F8)
        tf[...] = cg[...] + lateral(yf[...], IM) + (yf[...] - sf[...])
        zf[...] = scan(tf[...], BWD, B2, True)
        complete(2 * t + 1, zf, plane_above, True, BP, B8)
        send_edge(t + 1, zf)
        if t == 0:
            prepare(1, coef_one)
            prepare(2, coef_two)

    up_recv[2] = zf[:, :, 0:1, :]
    low_recv[1] = zf[:, :, planes - 1:planes, :]

    @pl.when(jnp.logical_not(is_low))
    def _():
        halo_copy(1, up_recv.at[2], up_recv.at[3], sub - 1).start()

    @pl.when(jnp.logical_not(is_high))
    def _():
        halo_copy(2, low_recv.at[1], low_recv.at[0], sub + 1).start()

    partial = right_side[...] - (apply(RAW, zf[...]) - lateral(zf[...], RAW + 1))
    height = rows * LANES
    r_row = lax.broadcasted_iota(jnp.int32, (height, LANES), 0)
    r_col = lax.broadcasted_iota(jnp.int32, (height, LANES), 1)
    half = BJ // 2
    share = (((r_row >> 5) * half) + ((r_row & (BJ - 1)) >> 1) == r_col).astype(jnp.float32)

    receive_edge(SWEEPS_FINE)

    @pl.when(is_low)
    def _():
        low_recv[0] = plane_below[...]

    @pl.when(is_high)
    def _():
        up_recv[3] = plane_above[...]

    @pl.when(jnp.logical_not(is_high))
    def _():
        halo_copy(1, up_recv.at[2], up_recv.at[3], sub).wait_recv()

    @pl.when(jnp.logical_not(is_low))
    def _():
        halo_copy(2, low_recv.at[1], low_recv.at[0], sub).wait_recv()

    lower = jnp.where(place == 0, low_recv[0], pltpu.roll(zf[...], 1, 2))
    upper = jnp.where(place == planes - 1, up_recv[3], pltpu.roll(zf[...], planes - 1, 2))
    residual = partial + apply(RAW + 5, lower) + apply(RAW + 6, upper)
    squares = jnp.sum((residual * residual).reshape(NV * rows, SUBLANES, LANES), axis=0)

    reduced = None
    for r in range(rows):
        term = jnp.dot(residual[:, r].reshape(NV * SUBLANES, LANES), share[r * LANES:(r + 1) * LANES],
                       precision=PRECISE, preferred_element_type=jnp.float32)
        reduced = term if reduced is None else reduced + term
    count = NV * planes // 2
    rsum[...] = reduced * 0.125
    gathered[sub, me, 0:count, :] = rsum[pl.ds(0, count, stride=2), :] + rsum[pl.ds(1, count, stride=2), :]
    gathered[sub, me, count:count + 1, :] = jnp.sum(squares, axis=0, keepdims=True)
    filler = gathered.shape[2] - count - 1
    gathered[sub, me, count + 1:, :] = jnp.zeros((filler, LANES), jnp.float32)

    def spread_copy(source, target):
        return pltpu.make_async_remote_copy(
            src_ref=gathered.at[sub, source], dst_ref=gathered.at[sub, source], send_sem=gs_sem.at[target],
            recv_sem=gr_sem.at[source], device_id=(target, sub), device_id_type=MESH)

    @pl.loop(1, blocks)
    def _(step):
        spread_copy(me, (me + step) % blocks).start()

    def across_copy(source, block, target):
        return pltpu.make_async_remote_copy(
            src_ref=gathered.at[source, block], dst_ref=gathered.at[source, block],
            send_sem=es_sem.at[target, block], recv_sem=er_sem.at[source, block],
            device_id=(me, target), device_id_type=MESH)

    for step in range(1, subs):
        across_copy(sub, me, (sub + step) % subs).start()

    @pl.loop(1, blocks)
    def _(step):
        source = (me + step) % blocks
        spread_copy(source, source).wait_recv()
        for turn in range(1, subs):
            across_copy(sub, source, (sub + turn) % subs).start()

    @pl.loop(0, blocks)
    def _(block):
        for turn in range(1, subs):
            source = (sub + turn) % subs
            across_copy(source, block, source).wait_recv()

    local = planes // 2
    total = jnp.zeros((1, LANES), jnp.float32)
    for s in range(subs):
        for a in range(NV):
            for k in range(local):
                field_f[a, s * local + k] = gathered[s, :, a * local + k, :]
        total = total + jnp.sum(gathered[s, :, count, :], axis=0, keepdims=True)

    def root_mean(value, entries):
        return jnp.sqrt(jnp.sum(value, axis=1, keepdims=True) / jnp.float32(entries))

    size = NV * blocks * subs * planes * rows * LANES
    norms[0:1, :] = jnp.broadcast_to(root_mean(total, size), (1, LANES))

    def level(store, cells, width, g, c, p, v, y, sweeps):
        depth = g.shape[1]
        inside = lane < cells
        mask_im = (lane >= width) & inside
        mask_ip = lane < cells - width
        mask_jm = ((lane & (width - 1)) != 0) & inside
        mask_jp = ((lane & (width - 1)) != width - 1) & inside
        bits = [1 << n for n in range(cells.bit_length() - 1)]
        bits_j = [n for n in bits if n < width]
        bits_i = [n for n in bits if n >= width]
        chunk = max(1, 4 * SUBLANES // blocks)

        def use(index, values):
            cut = values.reshape(NV, -1, SUBLANES, LANES)
            terms = [store[index, b][:, None] * cut[b][None] for b in range(NV)]
            out = (terms[0] + terms[1]) + (terms[2] + terms[3]) + terms[4]
            return out.reshape(values.shape)

        def sides(values, base):
            axis = values.ndim - 1
            out = use(base, jnp.where(mask_im, pltpu.roll(values, width, axis), 0.0))
            out = out + use(base + 1, jnp.where(mask_ip, pltpu.roll(values, LANES - width, axis), 0.0))
            out = out + use(base + 2, jnp.where(mask_jm, pltpu.roll(values, 1, axis), 0.0))
            return out + use(base + 3, jnp.where(mask_jp, pltpu.roll(values, LANES - 1, axis), 0.0))

        def flipped(values, odd, high):
            swapped = values
            for bit in bits_i:
                swapped = lane_xor(swapped, bit)
            values = jnp.where(odd, swapped, values)
            swapped = values
            for bit in bits_j:
                swapped = lane_xor(swapped, bit)
            return jnp.where(high, swapped, values)

        slot = lax.broadcasted_iota(jnp.int32, (blocks, 1), 0)

        def codes(source):
            out = jnp.zeros((blocks, 1), jnp.int32)
            for n in range(blocks):
                out = jnp.where(slot == n, source(n), out)
            return out

        code_below = codes(lambda n: orient[down[n]])
        code_above = codes(lambda n: orient[n])

        def interfaces():
            below = jnp.concatenate([v[:, depth - 1, pl.ds(down[n], 1), :] for n in range(blocks)], axis=1)
            above = jnp.concatenate([v[:, 0, pl.ds(partner[n], 1), :] for n in range(blocks)], axis=1)
            below = flipped(below, (code_below & 1) != 0, code_below >= 2)
            above = flipped(above, (code_above & 1) != 0, code_above >= 2)
            return below, above

        @pl.loop(0, depth // chunk)
        def _(step):
            at = pl.ds(step * chunk, chunk)
            c[:, at] = use(INV, g[:, at])

        nothing = jnp.zeros((NV, blocks, LANES), jnp.float32)
        below, above = nothing, nothing
        for n in range(sweeps):
            if n > 0:
                below, above = interfaces()
                p[:, depth - 1] = use(BWD, above)

            def forward(step, previous):
                at = pl.ds(step * chunk, chunk)
                s = c[:, at]
                if n > 0:
                    s = s + sides(v[:, at], IM) + p[:, at]
                made = []
                for u in range(chunk):
                    behind = use(FWD, previous)
                    previous = s[:, u] + behind
                    made.append((previous, behind))
                for u, (now, behind) in enumerate(made):
                    y[:, step * chunk + u] = now
                    p[:, step * chunk + u] = behind
                return previous

            lax.fori_loop(0, depth // chunk, forward, below)

            def backward(step, following):
                start = depth - chunk - step * chunk
                at = pl.ds(start, chunk)
                t = c[:, at] + sides(y[:, at], IM) + p[:, at]
                made = []
                for u in range(chunk - 1, -1, -1):
                    ahead = use(BWD, following)
                    following = t[:, u] + ahead
                    made.append((u, following, ahead))
                for u, now, ahead in made:
                    v[:, start + u] = now
                    p[:, start + u] = ahead
                return following

            lax.fori_loop(0, depth // chunk, backward, above)
        below, above = interfaces()
        y[:, 0] = below

        @pl.loop(1, depth)
        def _(k):
            y[:, k] = v[:, k - 1]

        p[:, depth - 1] = above

        @pl.loop(0, depth - 1)
        def _(k):
            p[:, k] = v[:, k + 1]

        def remain(step, squares):
            at = pl.ds(step * chunk, chunk)
            now = v[:, at]
            image = use(RAW, now) - sides(now, RAW + 1) - use(RAW + 5, y[:, at]) - use(RAW + 6, p[:, at])
            out = g[:, at] - image
            c[:, at] = out
            return squares + jnp.sum(out * out, axis=1)

        squares = lax.fori_loop(0, depth // chunk, remain, nothing)
        return jnp.sum(squares.reshape(NV * blocks, LANES), axis=0, keepdims=True)

    depth_one = field_f.shape[1]
    cells_one = rows * LANES // 4
    total = level(coef_one, cells_one, BJ // 2, field_f, field_c, field_p, field_v, field_y, SWEEPS_MID)
    norms[1:2, :] = jnp.broadcast_to(root_mean(total, size // 8), (1, LANES))

    s_row = lax.broadcasted_iota(jnp.int32, (LANES, LANES), 0)
    s_col = lax.broadcasted_iota(jnp.int32, (LANES, LANES), 1)
    fold = (((s_row >> 4) * (BJ // 4)) + ((s_row & (BJ // 2 - 1)) >> 1) == s_col).astype(jnp.float32)
    depth_two = depth_one // 2

    @pl.loop(0, depth_two)
    def _(k):
        pair = (field_c[:, 2 * k] + field_c[:, 2 * k + 1]) * 0.125
        two_f[:, k] = jnp.dot(pair.reshape(NV * blocks, LANES), fold, precision=PRECISE,
                              preferred_element_type=jnp.float32).reshape(NV, blocks, LANES)

    total = level(coef_two, cells_one // 4, BJ // 4, two_f, two_c, two_p, two_v, two_y, SWEEPS_COARSE)
    norms[2:3, :] = jnp.broadcast_to(root_mean(total, size // 64), (1, LANES))

    unfold = (((s_col >> 4) * (BJ // 4)) + ((s_col & (BJ // 2 - 1)) >> 1) == s_row).astype(jnp.float32)

    @pl.loop(0, depth_two)
    def _(k):
        grown = jnp.dot(two_v[:, k].reshape(NV * blocks, LANES), unfold, precision=PRECISE,
                        preferred_element_type=jnp.float32).reshape(NV, blocks, LANES)
        field_v[:, 2 * k] = field_v[:, 2 * k] + grown
        field_v[:, 2 * k + 1] = field_v[:, 2 * k + 1] + grown

    for a in range(NV):
        for k in range(local):
            row = field_v[a, sub * local + k, pl.ds(me, 1), :]
            spread[pl.ds(a * planes + 2 * k, 2), :] = jnp.broadcast_to(row, (2, LANES))
            out_one[a, pl.ds(k, 1), :] = field_v[a, sub * local + k, pl.ds(held[0], 1), :]
        for k in range(local // 2):
            out_two[a, pl.ds(k, 1), :] = two_v[a, sub * (local // 2) + k, pl.ds(held[1], 1), :]

    c_row = lax.broadcasted_iota(jnp.int32, (LANES, LANES), 0)
    c_col = lax.broadcasted_iota(jnp.int32, (LANES, LANES), 1)
    for r in range(rows):
        grow = ((((c_col + r * LANES) >> 5) * half) + ((c_col & (BJ - 1)) >> 1) == c_row).astype(jnp.float32)
        grown = jnp.dot(spread[...], grow, precision=PRECISE, preferred_element_type=jnp.float32)
        corrected[:, r] = zf[:, r] + grown.reshape(NV, SUBLANES, LANES)

    for t in range(SWEEPS_FINE + 1):
        @pl.when(is_low | is_high)
        def _():
            @pl.loop(0, blocks)
            def _(b):
                edge_copy(t, b).wait_send()

    @pl.when(jnp.logical_not(is_low))
    def _():
        halo_copy(0, up_recv.at[1], up_recv.at[0], sub - 1).wait_send()
        halo_copy(1, up_recv.at[2], up_recv.at[3], sub - 1).wait_send()

    @pl.when(jnp.logical_not(is_high))
    def _():
        halo_copy(2, low_recv.at[1], low_recv.at[0], sub + 1).wait_send()

    for n in range(2 * SWEEPS_FINE):
        for target in range(subs):
            @pl.when((target < sub) if n % 2 else (target > sub))
            def _():
                prefix_copy(n, sub, target).wait_send()

    @pl.loop(1, blocks)
    def _(step):
        spread_copy(me, (me + step) % blocks).wait_send()

    @pl.loop(0, blocks)
    def _(block):
        for turn in range(1, subs):
            across_copy(sub, block, (sub + turn) % subs).wait_send()


def shards(solution, right_side, couple, partner, orient, owner_one, owner_two):
    blocks = lax.axis_size("blk")
    subs = lax.axis_size("sub")
    planes, cells = solution.shape[2:]
    rows = cells // LANES
    tall = planes * subs

    def tiled(x):
        return x.reshape(NV, planes, rows, LANES).transpose(0, 2, 1, 3)

    vmem = pl.BlockSpec(memory_space=pltpu.VMEM)
    smem = pl.BlockSpec(memory_space=pltpu.SMEM)
    f32 = jnp.float32
    fine = pltpu.VMEM((NV, rows, planes, LANES), f32)
    plane = (NV, rows, 1, LANES)
    mid = pltpu.VMEM((NV, tall // 2, blocks, LANES), f32)
    low = pltpu.VMEM((NV, tall // 4, blocks, LANES), f32)
    matrix = (NV, NV, SUBLANES, LANES)
    payload = NV * planes // 2 + 4
    dma = pltpu.SemaphoreType.DMA
    edges = SWEEPS_FINE + 1
    corrected, one, two, norms = pl.pallas_call(
        functools.partial(kernel, (blocks, subs)),
        name="vcycle",
        out_shape=(
            jax.ShapeDtypeStruct((NV, rows, planes, LANES), f32),
            jax.ShapeDtypeStruct((NV, planes // 2, LANES), f32),
            jax.ShapeDtypeStruct((NV, planes // 4, LANES), f32),
            jax.ShapeDtypeStruct((3, LANES), f32),
        ),
        in_specs=[vmem, vmem, smem, smem, smem, smem, smem],
        out_specs=(vmem, vmem, vmem, vmem),
        scratch_shapes=[
            pltpu.VMEM((22,) + matrix, f32), pltpu.VMEM((14,) + matrix, f32), pltpu.VMEM((14,) + matrix, f32),
            fine, fine, fine, fine, fine,
            pltpu.VMEM(plane, f32), pltpu.VMEM(plane, f32), pltpu.VMEM(plane, f32),
            pltpu.VMEM((edges,) + plane, f32), *[pltpu.VMEM((blocks,) + plane, f32)] * edges,
            pltpu.VMEM((4,) + plane, f32), pltpu.VMEM((2,) + plane, f32),
            pltpu.VMEM((2 * SWEEPS_FINE, subs) + plane, f32),
            pltpu.VMEM((subs, blocks, payload, LANES), f32),
            pltpu.VMEM((NV * planes, LANES), f32),
            pltpu.SMEM((blocks,), jnp.int32),
            mid, mid, mid, mid, mid, low, low, low, low, low,
            pltpu.VMEM((NV * planes, LANES), f32),
            dma((edges, blocks)), dma((edges, blocks)), dma((3,)), dma((3,)),
            dma((2 * SWEEPS_FINE, subs)), dma((2 * SWEEPS_FINE, subs)),
            dma((blocks,)), dma((blocks,)), dma((subs, blocks)), dma((subs, blocks)),
        ],
        compiler_params=pltpu.CompilerParams(has_side_effects=True, vmem_limit_bytes=60 * 1024 * 1024),
    )(tiled(solution), tiled(right_side), couple.reshape(-1), partner, orient, owner_one, owner_two)
    corrected = corrected.transpose(0, 2, 1, 3).reshape(NV, 1, planes, cells)
    one = one.reshape(NV, 1, planes // 2, cells // 4)
    two = two[:, None, :, :cells // 16]
    return (corrected, one, two, norms[:, 0])


def solution(mesh):
    split = P(None, "blk", "sub", None)
    return jax.shard_map(
        shards,
        mesh=mesh,
        in_specs=(split, split, P(), P(), P(), P(), P()),
        out_specs=(split, split, split, P()),
        check_vma=False,
    )
```

profile of v0, /device:TPU:0, one launch (start us, length us, event | category | flops | bytes accessed | tf_op | source)
XLA Modules:
  0.0 65.5 jit_solution(9243148805622014192)
XLA Ops:
  0.6 1.1 %copy.13 = f32[3,7,5,5]{3,2,1,0:T(8,128)S(1)} copy(f32[3,7,5,5]{1,0,3,2:T(4,128)} %param.9) | data formatting | bytes 4200 | tf_op args[2]
  1.7 0.8 %reshape.25.couple = f32[525]{0:T(1024)} reshape(f32[3,7,5,5]{3,2,1,0:T(8,128)S(1)} %copy.13) | data formatting | bytes 4200 | tf_op jit(solution)/shard_map/reshape | solution.py:613
  2.5 59.0 %vcycle.1 = (f32[5,4,8,128]{3,2,1,0:T(8,128)}, f32[5,4,128]{2,1,0:T(4,128)}, f32[5,2,128]{2,1,0:T(2,128)}, f32[3,128]{1,0:T(4,128)}) custom-call(f32[5,4,8,128]{3,2,1,0:T(8,128)} %bitcast.16, f32[5,4,8,128]{3,2,1,0:T(8,128)} %bitcast.17, f32[525]{0:T(1024)} %reshape.25.couple, s32[8]{0:T(128)} %partner.1, s32[8]{0:T(128)} %orient.1, s32[8]{0:T(128)} %owner_one.1, ...), custom_call_target="tpu_custom_call" | custom-call | tf_op jit(solution)/shard_map/vcycle/pallas_call | solution.py:585
  61.5 0.0 copy-start.1
  61.5 0.0 copy-start.2
  61.5 0.7 %copy-done.2 = f32[3,128]{1,0:T(4,128)S(1)} copy-done((f32[3,128]{1,0:T(4,128)S(1)}, f32[3,128]{1,0:T(4,128)}, u32[]{:S(2)}) %copy-start.2) | copy-done | bytes 1560
  62.2 0.6 slice_reduce_fusion
  62.8 0.0 copy-done.1
  62.8 0.6 slice_bitcast_fusion
  63.4 0.0 copy-start
  63.4 1.5 %copy.18 = f32[5,1,8,512]{3,2,1,0:T(8,128)} copy(f32[5,1,8,512]{3,2,1,0:T(8,128)} %bitcast.18) | data formatting | bytes 163840
  64.9 0.0 copy-done
  64.9 0.6 copy.19
Async XLA Ops:
  61.5 1.3 %copy-start.1 = (f32[5,2,128]{2,1,0:T(2,128)S(1)}, f32[5,2,128]{2,1,0:T(2,128)}, u32[]{:S(2)}) copy-start(f32[5,2,128]{2,1,0:T(2,128)} %get-tuple-element.10) | copy-start | bytes 15364
  61.5 0.7 %copy-start.2 = (f32[3,128]{1,0:T(4,128)S(1)}, f32[3,128]{1,0:T(4,128)}, u32[]{:S(2)}) copy-start(f32[3,128]{1,0:T(4,128)} %get-tuple-element.11) | copy-start | bytes 4612
  63.4 1.5 %copy-start = (f32[5,4,128]{2,1,0:T(4,128)S(1)}, f32[5,4,128]{2,1,0:T(4,128)}, u32[]{:S(2)}) copy-start(f32[5,4,128]{2,1,0:T(4,128)} %get-tuple-element.9) | copy-start | bytes 30724
where the time goes:
time: 65.8 us; the launch traced here: 65.5 us
  Pallas kernels  59 us (90%)
  local copies, waits for them, and re-layouts  5.88 us (9%)
  between operations  0.66 us (1%)
    pallas_call x1, Pallas kernels, shards(): pl.pallas_call(functools.partial(kernel, (blocks, subs)), name='vcycle',...  59 us
    unnamed x10, local copies, waits for them, and re-layouts  4.48 us

commit v1 on v0

--- a/solution.py
+++ b/solution.py
@@ -119,12 +119,13 @@
             src_ref=prefix.at[n, source], dst_ref=prefix.at[n, source], send_sem=ps_sem.at[n, target],
             recv_sem=pr_sem.at[n, source], device_id=(me, target), device_id_type=MESH)
 
-    send_edge(0, solution)
-    up_recv[1] = solution[:, :, 0:1, :]
-
-    @pl.when(jnp.logical_not(is_low))
-    def _():
-        halo_copy(0, up_recv.at[1], up_recv.at[0], sub - 1).start()
+    here = me * subs + sub
+
+    @pl.loop(1, blocks * subs)
+    def _(step):
+        there = (here + step) % (blocks * subs)
+        pl.semaphore_signal(pltpu.get_barrier_semaphore(), inc=1,
+                            device_id=(there // subs, there % subs), device_id_type=MESH)
 
     def found(mapping, value):
         return lax.fori_loop(0, blocks, lambda n, best: jnp.where(mapping[n] == value, n, best), 0)
@@ -136,9 +137,8 @@
     held = (found(owner_one, me), found(owner_two, me))
 
     def splat(level, matrix):
-        base = (level * 7 + matrix) * NV * NV
         return jnp.stack([
-            jnp.stack([jnp.full((SUBLANES, LANES), couple[base + a * NV + b], jnp.float32) for a in range(NV)])
+            jnp.stack([jnp.full((SUBLANES, LANES), couple[a, b, level, matrix], jnp.float32) for a in range(NV)])
             for b in range(NV)
         ])
 
@@ -233,8 +233,15 @@
                     enter[...] = prefix[n, source] + apply(index_block, enter[...], 1)
             ref[...] = ref[...] + apply(index_all, enter[...])
 
+    up_recv[1] = solution[:, :, 0:1, :]
     cg[...] = apply(INV, right_side[...])
     sf[...] = cg[...] + lateral(solution[...], IM)
+    pl.semaphore_wait(pltpu.get_barrier_semaphore(), blocks * subs - 1)
+    send_edge(0, solution)
+
+    @pl.when(jnp.logical_not(is_low))
+    def _():
+        halo_copy(0, up_recv.at[1], up_recv.at[0], sub - 1).start()
     for t in range(SWEEPS_FINE):
         if t > 0:
             sf[...] = cg[...] + lateral(zf[...], IM) + (zf[...] - tf[...])
@@ -559,6 +566,15 @@
     def _(block):
         for turn in range(1, subs):
             across_copy(sub, block, (sub + turn) % subs).wait_send()
+
+
+def finish(corrected, one, two, norms, out, out_one, out_two, out_norms):
+    for r in range(corrected.shape[1]):
+        out[:, 0, :, r * LANES:(r + 1) * LANES] = corrected[:, r]
+    out_one[:, 0] = one[...]
+    out_two[:, 0] = two[:, :, :out_two.shape[3]]
+    for n in range(3):
+        out_norms[n] = jnp.max(norms[n:n + 1, :])
 
 
 def shards(solution, right_side, couple, partner, orient, owner_one, owner_two):
@@ -586,10 +602,10 @@
         functools.partial(kernel, (blocks, subs)),
         name="vcycle",
         out_shape=(
-            jax.ShapeDtypeStruct((NV, rows, planes, LANES), f32),
-            jax.ShapeDtypeStruct((NV, planes // 2, LANES), f32),
-            jax.ShapeDtypeStruct((NV, planes // 4, LANES), f32),
-            jax.ShapeDtypeStruct((3, LANES), f32),
+            pltpu.VMEM((NV, rows, planes, LANES), f32),
+            pltpu.VMEM((NV, planes // 2, LANES), f32),
+            pltpu.VMEM((NV, planes // 4, LANES), f32),
+            pltpu.VMEM((3, LANES), f32),
         ),
         in_specs=[vmem, vmem, smem, smem, smem, smem, smem],
         out_specs=(vmem, vmem, vmem, vmem),
@@ -609,12 +625,21 @@
             dma((2 * SWEEPS_FINE, subs)), dma((2 * SWEEPS_FINE, subs)),
             dma((blocks,)), dma((blocks,)), dma((subs, blocks)), dma((subs, blocks)),
         ],
-        compiler_params=pltpu.CompilerParams(has_side_effects=True, vmem_limit_bytes=60 * 1024 * 1024),
-    )(tiled(solution), tiled(right_side), couple.reshape(-1), partner, orient, owner_one, owner_two)
-    corrected = corrected.transpose(0, 2, 1, 3).reshape(NV, 1, planes, cells)
-    one = one.reshape(NV, 1, planes // 2, cells // 4)
-    two = two[:, None, :, :cells // 16]
-    return (corrected, one, two, norms[:, 0])
+        compiler_params=pltpu.CompilerParams(collective_id=0, has_side_effects=True, vmem_limit_bytes=60 * 1024 * 1024),
+    )(tiled(solution), tiled(right_side), couple.transpose(2, 3, 0, 1), partner, orient, owner_one, owner_two)
+    corrected, one, two, norms = pl.pallas_call(
+        finish,
+        name="finish",
+        out_shape=(
+            jax.ShapeDtypeStruct((NV, 1, planes, cells), f32),
+            jax.ShapeDtypeStruct((NV, 1, planes // 2, cells // 4), f32),
+            jax.ShapeDtypeStruct((NV, 1, planes // 4, cells // 16), f32),
+            jax.ShapeDtypeStruct((3,), f32),
+        ),
+        in_specs=[vmem] * 4,
+        out_specs=(vmem, vmem, vmem, smem),
+    )(*[pltpu.with_memory_space_constraint(x, pltpu.VMEM) for x in (corrected, one, two, norms)])
+    return corrected, one, two, norms
 
 
 def solution(mesh):

time: 65.8 us -> 57.4 us (0.87)
  local copies, waits for them, and re-layouts: 5.88 us -> 0 us
  Pallas kernels: 59 us -> 56.5 us
    unnamed x10 -> x0, local copies, waits for them, and re-layouts: 4.48 us -> none
    pallas_call x1, Pallas kernels: 59 us -> 55.9 us  [shards(): pl.pallas_call(functools.partial(kernel, (blocks, subs)), name='vcycle',...]
    reshape x1 -> x0, local copies, waits for them, and re-layouts: 0.78 us -> none  [shards(): couple.reshape(-1)]
where the time goes in v1:
time: 57.4 us; the launch traced here: 57.2 us
  Pallas kernels  56.5 us (98%)
  between operations  0.64 us (1%)
    pallas_call x1, Pallas kernels, shards(): pl.pallas_call(functools.partial(kernel, (blocks, subs)), name='vcycle',...  55.9 us

profile of v1, /device:TPU:0, one launch (start us, length us, event | category | flops | bytes accessed | tf_op | source)
XLA Modules:
  0.0 57.2 jit_solution(10033372329075822808)
XLA Ops:
  0.6 55.9 %vcycle.1 = (f32[5,4,8,128]{3,2,1,0:T(8,128)S(1)}, f32[5,4,128]{2,1,0:T(4,128)S(1)}, f32[5,2,128]{2,1,0:T(2,128)S(1)}, f32[3,128]{1,0:T(4,128)S(1)}) custom-call(f32[5,4,8,128]{3,2,1,0:T(8,128)} %bitcast.7, f32[5,4,8,128]{3,2,1,0:T(8,128)} %bitcast.8, f32[5,5,3,7]{3,2,1,0:T(4,128)} %bitcast.9, s32[8]{0:T(128)} %partner.1, s32[8]{0:T(128)} %orient.1, ...), custom_call_target="tpu_custom_call" | custom-call | tf_op jit(solution)/shard_map/vcycle/pallas_call | solution.py:601
  56.5 0.7 %finish.1 = (f32[5,1,8,512]{3,2,1,0:T(8,128)}, f32[5,1,4,128]{3,2,1,0:T(4,128)}, f32[5,1,2,32]{3,2,1,0:T(2,128)}, f32[3]{0:T(128)}) custom-call(f32[5,4,8,128]{3,2,1,0:T(8,128)S(1)} %get-tuple-element.8.corrected, f32[5,4,128]{2,1,0:T(4,128)S(1)} %get-tuple-element.9.one, f32[5,2,128]{2,1,0:T(2,128)S(1)} %get-tuple-element.10.two, ...), custom_call_target="tpu_custom_call" | custom-call | tf_op jit(solution)/shard_map/finish/pallas_call | solution.py:630

commit v2 on v1

v2 whole, which is shorter than its diff:
```python
import functools

import jax
import jax.numpy as jnp
from jax import lax
from jax.experimental import pallas as pl
from jax.experimental.pallas import tpu as pltpu
from jax.sharding import PartitionSpec as P

BI = 32
BJ = 16
SWEEPS_FINE = 2
SWEEPS_MID = 2
SWEEPS_COARSE = 4
LANES = 128
SUBLANES = 8
NV = 5
MESH = pl.DeviceIdType.MESH

RAW = 0
INV, IM, IP, JM, JP, FWD, BWD = 7, 8, 9, 10, 11, 12, 13
F2, F4, F8, FP, B2, B4, B8, BP = 14, 15, 16, 17, 18, 19, 20, 21
F16, B16, G0, G1 = 22, 23, 24, 25


def product(left, right):
    total = left[0][None] * right[:, 0][:, None]
    for b in range(1, NV):
        total = total + left[b][None] * right[:, b][:, None]
    return total


def permute(values, places):
    flat = values.reshape(-1, LANES)
    index = jnp.broadcast_to(places, values.shape).reshape(-1, LANES)
    return jnp.take_along_axis(flat, index, axis=1, mode="promise_in_bounds").reshape(values.shape)


def halves(values):
    high = values.astype(jnp.bfloat16)
    return high, (values - high.astype(jnp.float32)).astype(jnp.bfloat16)


def chosen(values, selection):
    high, low = halves(values)
    picks = selection.astype(jnp.bfloat16)
    return (jnp.dot(high, picks, preferred_element_type=jnp.float32)
            + jnp.dot(low, picks, preferred_element_type=jnp.float32))


def kernel(
    sizes, solution, right_side, couple, partner, orient, owner_one, owner_two,
    corrected, out_one, out_two, norms,
    coef, coef_one, coef_two, cg, sf, yf, tf, zf, wide, old_above,
    xsend, *more,
):
    edges = SWEEPS_FINE + 1
    edge_w, edge_a, more = more[:edges], more[edges:2 * edges], more[2 * edges:]
    (
        starts, prefix, gathered, rsum, low_recv, squares_recv,
        down,
        field_f, field_c, field_p, field_v, field_y,
        two_f, two_c, two_p, two_v, two_y, spread,
        xs_sem, xw_sem, xa_sem, us_sem, ur_sem, ps_sem, pr_sem, gs_sem, gr_sem, es_sem, er_sem,
        hs_sem, hr_sem, ns_sem, nr_sem,
    ) = more
    blocks, subs = sizes
    me = lax.axis_index("blk")
    sub = lax.axis_index("sub")
    last = subs - 1
    is_low = sub == 0
    is_high = sub == last
    rows = solution.shape[1]
    planes = SUBLANES
    count_all = blocks * subs
    here = me * subs + sub

    @pl.loop(1, count_all)
    def _(step):
        there = (here + step) % count_all
        pl.semaphore_signal(pltpu.get_barrier_semaphore(), inc=1,
                            device_id=(there // subs, there % subs), device_id_type=MESH)

    def found(mapping, value):
        return lax.fori_loop(0, blocks, lambda n, best: jnp.where(mapping[n] == value, n, best), 0)

    @pl.loop(0, blocks)
    def _(n):
        down[n] = found(partner, n)

    held = (found(owner_one, me), found(owner_two, me))
    lane = lax.broadcasted_iota(jnp.int32, (1, LANES), 1)
    place = lax.broadcasted_iota(jnp.int32, (SUBLANES, LANES), 0)

    def edge_copy(n, b, t, kind, source):
        edge = edge_a if kind else edge_w
        return pltpu.make_async_remote_copy(
            src_ref=xsend.at[n], dst_ref=edge[n].at[source], send_sem=xs_sem.at[n, b, t],
            recv_sem=(xa_sem if kind else xw_sem).at[n, source], device_id=(b, t), device_id_type=MESH)

    def targets(n, kind):
        if n < SWEEPS_FINE:
            return (0, last) + tuple(range(1, last))
        return (last,) if kind else (0,)

    def send_edge(n, ref):
        code = jnp.where(is_low, orient[down[me]], orient[me])
        turned = permute(ref[...], lane ^ jnp.where(code // 2 == 1, BJ - 1, 0) ^ jnp.where(code % 2 == 1, LANES - BJ, 0))
        swapped = jnp.concatenate([turned[:, r:r + 1] for r in range(rows - 1, -1, -1)], axis=1)
        turned = jnp.where(code % 2 == 1, swapped, turned)

        for kind, mine in ((1, is_low), (0, is_high)):
            @pl.when(mine)
            def _():
                edge = edge_a if kind else edge_w
                at = 0 if kind else planes - 1
                xsend[n] = turned[:, :, at:at + 1]
                edge[n][me] = turned[:, :, at:at + 1]
                own = 0 if kind else last
                for t in targets(n, kind):
                    first = 1 if t == own else 0

                    @pl.loop(first, blocks)
                    def _(step):
                        edge_copy(n, (me + step) % blocks, t, kind, me).start()

    def receive_edge(n):
        for kind in (0, 1):
            own = 0 if kind else last
            for t in range(subs):
                if t not in targets(n, kind):
                    continue
                first = 1 if t == own else 0

                @pl.when(sub == t)
                def _():
                    @pl.loop(first, blocks)
                    def _(step):
                        source = (me + step) % blocks
                        edge_copy(n, source, t, kind, source).wait_recv()

    def start_copy(source, target):
        return pltpu.make_async_remote_copy(
            src_ref=starts.at[source], dst_ref=starts.at[source], send_sem=us_sem.at[target],
            recv_sem=ur_sem.at[source], device_id=(me, target), device_id_type=MESH)

    def prefix_copy(n, source, target):
        return pltpu.make_async_remote_copy(
            src_ref=prefix.at[n, source], dst_ref=prefix.at[n, source], send_sem=ps_sem.at[n, target],
            recv_sem=pr_sem.at[n, source], device_id=(me, target), device_id_type=MESH)

    def splat(level, matrix):
        return jnp.stack([
            jnp.stack([jnp.full((SUBLANES, LANES), couple[a, b, level, matrix], jnp.float32) for a in range(NV)])
            for b in range(NV)
        ])

    identity = jnp.stack([
        jnp.stack([jnp.full((SUBLANES, LANES), 1.0 if a == b else 0.0, jnp.float32) for a in range(NV)])
        for b in range(NV)
    ])

    def prepare(level, store):
        for matrix in range(7):
            store[RAW + matrix] = splat(level, matrix)
        store[INV] = identity

        @pl.loop(0, 6)
        def _(repeat):
            approx = store[INV]
            store[INV] = product(approx, 2.0 * identity - product(store[RAW], approx))

        @pl.loop(0, 6)
        def _(matrix):
            store[IM + matrix] = product(store[INV], store[RAW + 1 + matrix])

    prepare(0, coef)

    def powers(base, second, sixteenth, count):
        coef[second] = product(coef[base], coef[base])
        coef[second + 1] = product(coef[second], coef[second])
        coef[second + 2] = product(coef[second + 1], coef[second + 1])
        coef[sixteenth] = product(coef[second + 2], coef[second + 2])
        run = jnp.where((count & 1) != 0, coef[base], identity)
        for bit, index in ((2, second), (4, second + 1), (8, second + 2)):
            run = product(jnp.where((count & bit) != 0, coef[index], identity), run)
        coef[second + 3] = run

    powers(FWD, F2, F16, place + 1)
    powers(BWD, B2, B16, planes - place)

    def combined():
        seventh = product(coef[B4], product(coef[B2], coef[BWD]))

        @pl.loop(0, NV)
        def _(n):
            middle = jnp.where(n == 0, identity, coef[jnp.maximum(IM + n - 1, IM)])
            total = product(middle, coef[FWD])
            for back, ahead in ((BWD, FWD), (B2, F2), (B4, F4)):
                total = total + product(coef[back], product(total, coef[ahead]))
            coef[G0 + n] = jnp.where(place < subs, total, product(seventh, middle))

    def apply(index, values, height=SUBLANES):
        total = None
        for b in range(NV):
            term = coef[index, b][:, None, :height] * values[b][None]
            total = term if total is None else total + term
        return total

    in_low = lane < BJ
    in_high = lane >= LANES - BJ
    j_first = (lane & (BJ - 1)) == 0
    j_final = (lane & (BJ - 1)) == BJ - 1

    def lateral(values, base):
        zero = jnp.zeros_like(values[:, :1])
        turned = pltpu.roll(values, BJ, 3)
        total = apply(base, jnp.where(in_low, jnp.concatenate([zero, turned[:, :-1]], axis=1), turned))
        turned = pltpu.roll(values, LANES - BJ, 3)
        total = total + apply(base + 1, jnp.where(in_high, jnp.concatenate([turned[:, 1:], zero], axis=1), turned))
        total = total + apply(base + 2, jnp.where(j_first, 0.0, pltpu.roll(values, 1, 3)))
        return total + apply(base + 3, jnp.where(j_final, 0.0, pltpu.roll(values, LANES - 1, 3)))

    def scan(values, indices, reverse, length=planes):
        by = 1
        for index in indices:
            if reverse:
                shifted = jnp.where(place < length - by, pltpu.roll(values, SUBLANES - by, 2), 0.0)
            else:
                shifted = jnp.where((place >= by) & (place < length), pltpu.roll(values, by, 2), 0.0)
            values = values + apply(index, shifted)
            by *= 2
        return values

    starts[sub] = solution[:, :, 0:1, :]
    cg[...] = apply(INV, right_side[...])
    upper = jnp.where(place == planes - 1, 0.0, pltpu.roll(solution[...], planes - 1, 2))
    sf[...] = cg[...] + lateral(solution[...], IM) + apply(BWD, upper)

    def local(n):
        yf[...] = scan(sf[...], (FWD, F2, F4), False)
        tf[...] = cg[...] + lateral(yf[...], IM) + (yf[...] - sf[...])
        part = scan(tf[...], (BWD, B2, B4), True)
        prefix[n, sub, 0] = yf[:, :, planes - 1:planes, :]
        prefix[n, sub, 1] = part[:, :, 0:1, :]

    def send_prefix(n):
        for target in range(subs):
            @pl.when(sub != target)
            def _():
                prefix_copy(n, sub, target).start()

    local(0)
    pl.semaphore_wait(pltpu.get_barrier_semaphore(), count_all - 1)
    send_edge(0, solution)
    for target in range(subs):
        @pl.when((sub > 0) & (sub != target))
        def _():
            start_copy(sub, target).start()
    send_prefix(0)
    combined()
    for number, store in ((1, coef_one), (2, coef_two)):
        prepare(number, store)
        width = BJ >> number
        cells = rows * LANES >> (2 * number)
        inside = lane < cells
        masks = ((lane >= width) & inside, lane < cells - width,
                 ((lane & (width - 1)) != 0) & inside, ((lane & (width - 1)) != width - 1) & inside)
        for shift, mask in enumerate(masks):
            for base in (RAW + 1, IM):
                store[base + shift] = jnp.where(mask, store[base + shift], 0.0)

    for n in range(SWEEPS_FINE):
        for source in range(subs):
            @pl.when(sub != source)
            def _():
                if n == 0 and source > 0:
                    start_copy(source, sub).wait_recv()
                prefix_copy(n, source, sub).wait_recv()
        receive_edge(n)
        below = edge_w[n][down[me]]
        above = edge_a[n][partner[me]]
        missing = above if n == 0 else above - old_above[...]
        ahead = jnp.where(place == subs + last, missing, 0.0)
        if n == 0:
            for s in range(last):
                ahead = jnp.where(place == subs + s, starts[s + 1], ahead)
        old_above[...] = above
        ahead = apply(BWD, ahead)
        enter = jnp.where(place == 0, below, 0.0)
        final = jnp.zeros_like(enter)
        for s in range(subs):
            if s < last:
                enter = jnp.where(place == s + 1, prefix[n, s, 0], enter)
            if s > 0:
                final = jnp.where(place == s, prefix[n, s, 1], final)
        moved = pltpu.roll(ahead, SUBLANES + 1 - subs, 2)
        enter = enter + jnp.where((place > 0) & (place < subs), moved, 0.0)
        enter = scan(enter, (F8, F16), False, subs)
        both = enter + ahead
        sides = lateral(both, G1)
        final = final + apply(G0, enter) + sides + pltpu.roll(sides, SUBLANES - subs, 2)
        final = jnp.where(place < last, pltpu.roll(final, SUBLANES - 1, 2), jnp.where(place == last, above, 0.0))
        final = scan(final, (B8, B16), True, subs)
        wide[0] = both
        wide[1] = final
        enter = wide[0, :, :, pl.ds(sub, 1), :]
        extra = jnp.where(place == planes - 1, wide[0, :, :, pl.ds(subs + sub, 1), :], 0.0)
        y = yf[...] + apply(FP, enter) + extra
        yf[...] = y
        tf[...] = cg[...] + lateral(y, IM) + (y - (sf[...] + extra))
        zf[...] = scan(tf[...], (BWD, B2, B4), True) + apply(BP, wide[1, :, :, pl.ds(sub, 1), :])
        if n + 1 < SWEEPS_FINE:
            send_edge(n + 1, zf)
            sf[...] = cg[...] + lateral(zf[...], IM) + (zf[...] - tf[...])
            local(n + 1)
            send_prefix(n + 1)

    change = zf[...] - yf[...]
    lower = jnp.where(place == 0, -wide[0, :, :, pl.ds(sub, 1), :], pltpu.roll(change, 1, 2))
    upper = jnp.where((place == planes - 1) & is_high, -old_above[...], 0.0)
    sf[...] = lateral(change, RAW + 1) + apply(RAW + 5, lower) + apply(RAW + 6, upper)

    height = rows * LANES
    r_row = lax.broadcasted_iota(jnp.int32, (height, LANES), 0)
    r_col = lax.broadcasted_iota(jnp.int32, (height, LANES), 1)
    half = BJ // 2
    share = ((((r_row >> 5) * half) + ((r_row & (BJ - 1)) >> 1)) == r_col).astype(jnp.float32)
    reduced = None
    for r in range(rows):
        both = jnp.concatenate([sf[:, r].reshape(NV * SUBLANES, LANES), zf[:, r].reshape(NV * SUBLANES, LANES)], axis=0)
        term = chosen(both, share[r * LANES:(r + 1) * LANES])
        reduced = term if reduced is None else reduced + term
    count = NV * planes // 2
    rsum[...] = reduced * 0.125
    gathered[sub, me, 0:count, :] = rsum[pl.ds(0, count, stride=2), :] + rsum[pl.ds(1, count, stride=2), :]
    tail = gathered.shape[2] - count - 2 * NV
    gathered[sub, me, count:count + NV, :] = rsum[pl.ds(NV * planes + planes - 1, NV, stride=planes), :]
    gathered[sub, me, count + NV:count + 2 * NV, :] = rsum[pl.ds(NV * planes, NV, stride=planes), :]
    gathered[sub, me, count + 2 * NV:, :] = jnp.zeros((tail, LANES), jnp.float32)

    def spread_copy(source, target):
        return pltpu.make_async_remote_copy(
            src_ref=gathered.at[sub, source], dst_ref=gathered.at[sub, source], send_sem=gs_sem.at[target],
            recv_sem=gr_sem.at[source], device_id=(target, sub), device_id_type=MESH)

    @pl.loop(1, blocks)
    def _(step):
        spread_copy(me, (me + step) % blocks).start()

    def across_copy(source, block, target):
        return pltpu.make_async_remote_copy(
            src_ref=gathered.at[source, block], dst_ref=gathered.at[source, block],
            send_sem=es_sem.at[target, block], recv_sem=er_sem.at[source, block],
            device_id=(me, target), device_id_type=MESH)

    for step in range(1, subs):
        across_copy(sub, me, (sub + step) % subs).start()

    @pl.loop(1, blocks)
    def _(step):
        source = (me + step) % blocks
        spread_copy(source, source).wait_recv()
        for turn in range(1, subs):
            across_copy(sub, source, (sub + turn) % subs).start()

    @pl.loop(0, blocks)
    def _(block):
        for turn in range(1, subs):
            source = (sub + turn) % subs
            across_copy(source, block, source).wait_recv()

    send_edge(SWEEPS_FINE, zf)
    low_recv[0] = zf[:, :, planes - 1:planes, :]

    def halo_copy(target):
        return pltpu.make_async_remote_copy(
            src_ref=low_recv.at[0], dst_ref=low_recv.at[1], send_sem=hs_sem.at[0], recv_sem=hr_sem.at[0],
            device_id=(me, target), device_id_type=MESH)

    @pl.when(jnp.logical_not(is_high))
    def _():
        halo_copy(sub + 1).start()

    def use(store, index, values):
        cut = values.reshape(NV, -1, SUBLANES, LANES)
        terms = [store[index, b][:, None] * cut[b][None] for b in range(NV)]
        out = (terms[0] + terms[1]) + (terms[2] + terms[3]) + terms[4]
        return out.reshape(values.shape)

    slot = lax.broadcasted_iota(jnp.int32, (blocks, 1), 0)

    def codes(source):
        out = jnp.zeros((blocks, 1), jnp.int32)
        for n in range(blocks):
            out = jnp.where(slot == n, source(n), out)
        return out

    code_below = codes(lambda n: orient[down[n]])
    code_above = codes(lambda n: orient[n])

    def turned(values, code, cells, width):
        high = jnp.where((code & 1) != 0, cells - width, 0)
        return permute(values, lane ^ high ^ jnp.where(code >= 2, width - 1, 0))

    local_planes = planes // 2
    cells_one = rows * LANES // 4

    def edge_rows(s, pick, first):
        return jnp.stack([
            jnp.concatenate([gathered[s, pl.ds(pick(n), 1), first + a, :] for n in range(blocks)], axis=0)
            for a in range(NV)])

    under = turned(edge_rows(last, lambda n: down[n], count), code_below, cells_one, BJ // 2)
    over = turned(edge_rows(0, lambda n: partner[n], count + NV), code_above, cells_one, BJ // 2)
    for s in range(subs):
        if s > 0:
            under = jnp.stack([gathered[s - 1, :, count + a, :] for a in range(NV)])
        under = use(coef, RAW + 5, under)
        for k in range(local_planes):
            value = jnp.stack([gathered[s, :, a * local_planes + k, :] for a in range(NV)])
            if k == 0:
                value = value + under
            if s == last and k == local_planes - 1:
                value = value + use(coef, RAW + 6, over)
            field_f[:, s * local_planes + k] = value

    def root_mean(value, entries):
        return jnp.sqrt(jnp.sum(value, axis=1, keepdims=True) / jnp.float32(entries))

    size = NV * blocks * subs * planes * rows * LANES

    def level(store, cells, width, g, c, p, v, y, sweeps):
        depth = g.shape[1]
        chunk = max(1, 4 * SUBLANES // blocks)
        steps = depth // chunk

        def repeat(body, start, number):
            return lax.fori_loop(0, number, body, start, unroll=blocks <= SUBLANES)

        def sides(values, base):
            axis = values.ndim - 1
            out = use(store, base, pltpu.roll(values, width, axis))
            out = out + use(store, base + 1, pltpu.roll(values, LANES - width, axis))
            out = out + use(store, base + 2, pltpu.roll(values, 1, axis))
            return out + use(store, base + 3, pltpu.roll(values, LANES - 1, axis))

        def interfaces():
            below = jnp.concatenate([v[:, depth - 1, pl.ds(down[n], 1), :] for n in range(blocks)], axis=1)
            above = jnp.concatenate([v[:, 0, pl.ds(partner[n], 1), :] for n in range(blocks)], axis=1)
            return turned(below, code_below, cells, width), turned(above, code_above, cells, width)

        def centre(step, carry):
            at = pl.ds(step * chunk, chunk)
            c[:, at] = use(store, INV, g[:, at])
            return carry

        repeat(centre, 0, steps)
        nothing = jnp.zeros((NV, blocks, LANES), jnp.float32)
        below, above = nothing, nothing
        for n in range(sweeps):
            if n > 0:
                below, above = interfaces()
                p[:, depth - 1] = use(store, BWD, above)

            def forward(step, previous):
                at = pl.ds(step * chunk, chunk)
                s = c[:, at]
                if n > 0:
                    s = s + sides(v[:, at], IM) + p[:, at]
                made = []
                for u in range(chunk):
                    behind = use(store, FWD, previous)
                    previous = s[:, u] + behind
                    made.append((previous, behind))
                for u, (now, behind) in enumerate(made):
                    y[:, step * chunk + u] = now
                    p[:, step * chunk + u] = behind
                return previous

            repeat(forward, below, steps)

            def backward(step, following):
                start = depth - chunk - step * chunk
                at = pl.ds(start, chunk)
                t = c[:, at] + sides(y[:, at], IM) + p[:, at]
                made = []
                for u in range(chunk - 1, -1, -1):
                    ahead = use(store, BWD, following)
                    following = t[:, u] + ahead
                    made.append((u, following, ahead))
                for u, now, ahead in made:
                    v[:, start + u] = now
                    p[:, start + u] = ahead
                return following

            repeat(backward, above, steps)

        new_below, new_above = interfaces()
        top = use(store, RAW + 6, new_above - above)

        def remain(step, carry, final=False):
            squares, previous = carry
            at = pl.ds(step * chunk, chunk)
            change = v[:, at] - y[:, at]
            shifted = jnp.stack([previous] + [change[:, u] for u in range(chunk - 1)], axis=1)
            out = sides(change, RAW + 1) + use(store, RAW + 5, shifted)
            if final:
                out = jnp.stack([out[:, u] for u in range(chunk - 1)] + [out[:, chunk - 1] + top], axis=1)
            c[:, at] = out
            return squares + jnp.sum(out * out, axis=1), change[:, chunk - 1]

        carry = repeat(remain, (nothing, new_below - below), steps - 1)
        squares, _ = remain(steps - 1, carry, True)
        return jnp.sum(squares.reshape(NV * blocks, LANES), axis=0, keepdims=True)

    depth_one = field_f.shape[1]
    total = level(coef_one, cells_one, BJ // 2, field_f, field_c, field_p, field_v, field_y, SWEEPS_MID)
    norms[1:2, :] = jnp.broadcast_to(root_mean(total, size // 8), (1, LANES))

    receive_edge(SWEEPS_FINE)

    @pl.when(is_low)
    def _():
        low_recv[1] = edge_w[SWEEPS_FINE][down[me]]

    @pl.when(is_high)
    def _():
        fresh = apply(RAW + 6, edge_a[SWEEPS_FINE][partner[me]], 1)
        sf[:, :, planes - 1:planes, :] = sf[:, :, planes - 1:planes, :] + fresh

    @pl.when(jnp.logical_not(is_low))
    def _():
        halo_copy(sub).wait_recv()

    sf[:, :, 0:1, :] = sf[:, :, 0:1, :] + apply(RAW + 5, low_recv[1], 1)
    residual = sf[...]
    squares_recv[here] = jnp.sum((residual * residual).reshape(NV * rows * SUBLANES, LANES), axis=0, keepdims=True)

    def norm_copy(source, target):
        return pltpu.make_async_remote_copy(
            src_ref=squares_recv.at[source], dst_ref=squares_recv.at[source], send_sem=ns_sem.at[target],
            recv_sem=nr_sem.at[source], device_id=(target // subs, target % subs), device_id_type=MESH)

    @pl.loop(1, count_all)
    def _(step):
        norm_copy(here, (here + step) % count_all).start()

    s_row = lax.broadcasted_iota(jnp.int32, (LANES, LANES), 0)
    s_col = lax.broadcasted_iota(jnp.int32, (LANES, LANES), 1)
    fold = ((((s_row >> 4) * (BJ // 4)) + ((s_row & (BJ // 2 - 1)) >> 1)) == s_col).astype(jnp.float32)
    depth_two = depth_one // 2

    pairs = jnp.stack([field_c[:, 2 * k] + field_c[:, 2 * k + 1] for k in range(depth_two)], axis=1)
    two_f[...] = chosen(pairs.reshape(-1, LANES) * 0.125, fold).reshape(two_f.shape)

    total = level(coef_two, cells_one // 4, BJ // 4, two_f, two_c, two_p, two_v, two_y, SWEEPS_COARSE)
    norms[2:3, :] = jnp.broadcast_to(root_mean(total, size // 64), (1, LANES))

    unfold = ((((s_col >> 4) * (BJ // 4)) + ((s_col & (BJ // 2 - 1)) >> 1)) == s_row).astype(jnp.float32)
    coarse_planes = local_planes // 2
    for which, block in enumerate((me, held[0])):
        for a in range(NV):
            for k in range(coarse_planes):
                row = (which * NV + a) * coarse_planes + k
                rsum[row:row + 1, :] = two_v[a, sub * coarse_planes + k, pl.ds(block, 1), :]
    for a in range(NV):
        for k in range(coarse_planes):
            out_two[a, pl.ds(k, 1), :] = two_v[a, sub * coarse_planes + k, pl.ds(held[1], 1), :]
    filled = -(-2 * NV * coarse_planes // SUBLANES) * SUBLANES
    rsum[0:filled, :] = chosen(rsum[0:filled, :], unfold)
    for a in range(NV):
        for k in range(local_planes):
            at = sub * local_planes + k
            mine = a * coarse_planes + k // 2
            row = field_v[a, at, pl.ds(me, 1), :] + rsum[mine:mine + 1, :]
            spread[pl.ds(a * planes + 2 * k, 2), :] = jnp.broadcast_to(row, (2, LANES))
            mine = mine + NV * coarse_planes
            out_one[a, pl.ds(k, 1), :] = field_v[a, at, pl.ds(held[0], 1), :] + rsum[mine:mine + 1, :]

    for r in range(rows):
        grow = ((((s_col + r * LANES) >> 5) * half) + ((s_col & (BJ - 1)) >> 1) == s_row).astype(jnp.float32)
        corrected[:, r] = zf[:, r] + chosen(spread[...], grow).reshape(NV, SUBLANES, LANES)

    @pl.loop(1, count_all)
    def _(step):
        source = (here + step) % count_all
        norm_copy(source, source).wait_recv()

    total = jnp.sum(squares_recv[...].reshape(count_all, LANES), axis=0, keepdims=True)
    norms[0:1, :] = jnp.broadcast_to(root_mean(total, size), (1, LANES))

    for n in range(SWEEPS_FINE + 1):
        for kind, mine in ((1, is_low), (0, is_high)):
            @pl.when(mine)
            def _():
                own = 0 if kind else last
                for t in targets(n, kind):
                    first = 1 if t == own else 0

                    @pl.loop(first, blocks)
                    def _(step):
                        edge_copy(n, (me + step) % blocks, t, kind, me).wait_send()

    for target in range(subs):
        @pl.when((sub > 0) & (sub != target))
        def _():
            start_copy(sub, target).wait_send()

        @pl.when(sub != target)
        def _():
            for n in range(SWEEPS_FINE):
                prefix_copy(n, sub, target).wait_send()

    @pl.when(jnp.logical_not(is_high))
    def _():
        halo_copy(sub + 1).wait_send()

    @pl.loop(1, blocks)
    def _(step):
        spread_copy(me, (me + step) % blocks).wait_send()

    @pl.loop(0, blocks)
    def _(block):
        for turn in range(1, subs):
            across_copy(sub, block, (sub + turn) % subs).wait_send()

    @pl.loop(1, count_all)
    def _(step):
        norm_copy(here, (here + step) % count_all).wait_send()


def finish(corrected, one, two, norms, out, out_one, out_two, out_norms):
    for r in range(corrected.shape[1]):
        out[:, 0, :, r * LANES:(r + 1) * LANES] = corrected[:, r]
    out_one[:, 0] = one[...]
    out_two[:, 0] = two[:, :, :out_two.shape[3]]
    for n in range(3):
        out_norms[n] = jnp.max(norms[n:n + 1, :])


def shards(solution, right_side, couple, partner, orient, owner_one, owner_two):
    blocks = lax.axis_size("blk")
    subs = lax.axis_size("sub")
    planes, cells = solution.shape[2:]
    rows = cells // LANES
    tall = planes * subs

    def tiled(x):
        return x.reshape(NV, planes, rows, LANES).transpose(0, 2, 1, 3)

    vmem = pl.BlockSpec(memory_space=pltpu.VMEM)
    smem = pl.BlockSpec(memory_space=pltpu.SMEM)
    f32 = jnp.float32
    fine = pltpu.VMEM((NV, rows, planes, LANES), f32)
    plane = (NV, rows, 1, LANES)
    mid = pltpu.VMEM((NV, tall // 2, blocks, LANES), f32)
    low = pltpu.VMEM((NV, tall // 4, blocks, LANES), f32)
    matrix = (NV, NV, SUBLANES, LANES)
    payload = -(-(NV * planes // 2 + 2 * NV) // SUBLANES) * SUBLANES
    dma = pltpu.SemaphoreType.DMA
    edges = SWEEPS_FINE + 1
    everyone = blocks * subs
    results = pl.pallas_call(
        functools.partial(kernel, (blocks, subs)),
        name="vcycle",
        out_shape=(
            pltpu.VMEM((NV, rows, planes, LANES), f32),
            pltpu.VMEM((NV, planes // 2, LANES), f32),
            pltpu.VMEM((NV, planes // 4, LANES), f32),
            pltpu.VMEM((3, LANES), f32),
        ),
        in_specs=[vmem, vmem, smem, smem, smem, smem, smem],
        out_specs=(vmem, vmem, vmem, vmem),
        scratch_shapes=[
            pltpu.VMEM((29,) + matrix, f32), pltpu.VMEM((14,) + matrix, f32), pltpu.VMEM((14,) + matrix, f32),
            fine, fine, fine, fine, fine, pltpu.VMEM((2, NV, rows, planes, LANES), f32), pltpu.VMEM(plane, f32),
            pltpu.VMEM((edges,) + plane, f32),
            *[pltpu.VMEM((blocks,) + plane, f32)] * (2 * edges),
            pltpu.VMEM((subs,) + plane, f32),
            pltpu.VMEM((SWEEPS_FINE, subs, 2) + plane, f32),
            pltpu.VMEM((subs, blocks, payload, LANES), f32),
            pltpu.VMEM((2 * NV * planes, LANES), f32),
            pltpu.VMEM((2,) + plane, f32),
            pltpu.VMEM((everyone, 1, LANES), f32),
            pltpu.SMEM((blocks,), jnp.int32),
            mid, mid, mid, mid, mid, low, low, low, low, low,
            pltpu.VMEM((NV * planes, LANES), f32),
            dma((edges, blocks, subs)), dma((edges, blocks)), dma((edges, blocks)),
            dma((subs,)), dma((subs,)),
            dma((SWEEPS_FINE, subs)), dma((SWEEPS_FINE, subs)),
            dma((blocks,)), dma((blocks,)), dma((subs, blocks)), dma((subs, blocks)),
            dma((1,)), dma((1,)), dma((everyone,)), dma((everyone,)),
        ],
        compiler_params=pltpu.CompilerParams(collective_id=0, has_side_effects=True, vmem_limit_bytes=60 * 1024 * 1024),
    )(tiled(solution), tiled(right_side), couple.transpose(2, 3, 0, 1), partner, orient, owner_one, owner_two)
    return pl.pallas_call(
        finish,
        name="finish",
        out_shape=(
            jax.ShapeDtypeStruct((NV, 1, planes, cells), f32),
            jax.ShapeDtypeStruct((NV, 1, planes // 2, cells // 4), f32),
            jax.ShapeDtypeStruct((NV, 1, planes // 4, cells // 16), f32),
            jax.ShapeDtypeStruct((3,), f32),
        ),
        in_specs=[vmem] * 4,
        out_specs=(vmem, vmem, vmem, smem),
    )(*[pltpu.with_memory_space_constraint(x, pltpu.VMEM) for x in results])


def solution(mesh):
    split = P(None, "blk", "sub", None)
    return jax.shard_map(
        shards,
        mesh=mesh,
        in_specs=(split, split, P(), P(), P(), P(), P()),
        out_specs=(split, split, split, P()),
        check_vma=False,
    )
```

time: 57.4 us -> 47.7 us (0.83)
  Pallas kernels: 56.5 us -> 46.8 us
    pallas_call x1, Pallas kernels: 55.9 us -> 46.2 us  [shards(): pl.pallas_call(functools.partial(kernel, (blocks, subs)), name='vcycle',...]
where the time goes in v2:
time: 47.7 us; the launch traced here: 47.5 us
  Pallas kernels  46.8 us (98%)
  between operations  0.64 us (1%)
    pallas_call x1, Pallas kernels, shards(): pl.pallas_call(functools.partial(kernel, (blocks, subs)), name='vcycle',...  46.2 us

profile of v2, /device:TPU:0, one launch (start us, length us, event | category | flops | bytes accessed | tf_op | source)
XLA Modules:
  0.0 47.5 jit_solution(13127887193988820367)
XLA Ops:
  0.6 46.2 %vcycle.1 = (f32[5,4,8,128]{3,2,1,0:T(8,128)S(1)}, f32[5,4,128]{2,1,0:T(4,128)S(1)}, f32[5,2,128]{2,1,0:T(2,128)S(1)}, f32[3,128]{1,0:T(4,128)S(1)}) custom-call(f32[5,4,8,128]{3,2,1,0:T(8,128)} %bitcast.7, f32[5,4,8,128]{3,2,1,0:T(8,128)} %bitcast.8, f32[5,5,3,7]{3,2,1,0:T(4,128)} %bitcast.9, s32[8]{0:T(128)} %partner.1, s32[8]{0:T(128)} %orient.1, ...), custom_call_target="tpu_custom_call" | custom-call | tf_op jit(solution)/shard_map/vcycle/pallas_call | solution.py:664
  46.8 0.7 %finish.1 = (f32[5,1,8,512]{3,2,1,0:T(8,128)}, f32[5,1,4,128]{3,2,1,0:T(4,128)}, f32[5,1,2,32]{3,2,1,0:T(2,128)}, f32[3]{0:T(128)}) custom-call(f32[5,4,8,128]{3,2,1,0:T(8,128)S(1)} %get-tuple-element.8.corrected, f32[5,4,128]{2,1,0:T(4,128)S(1)} %get-tuple-element.9.one, f32[5,2,128]{2,1,0:T(2,128)S(1)} %get-tuple-element.10.two, ...), custom_call_target="tpu_custom_call" | custom-call | tf_op jit(solution)/shard_map/finish/pallas_call | solution.py:697

commit v3 on v2

--- a/solution.py
+++ b/solution.py
@@ -49,7 +49,7 @@
 
 
 def kernel(
-    sizes, solution, right_side, couple, partner, orient, owner_one, owner_two,
+    sizes, solution_hbm, right_side_hbm, couple_hbm, partner_hbm, orient_hbm, owner_one_hbm, owner_two_hbm,
     corrected, out_one, out_two, norms,
     coef, coef_one, coef_two, cg, sf, yf, tf, zf, wide, old_above,
     xsend, *more,
@@ -62,7 +62,7 @@
         field_f, field_c, field_p, field_v, field_y,
         two_f, two_c, two_p, two_v, two_y, spread,
         xs_sem, xw_sem, xa_sem, us_sem, ur_sem, ps_sem, pr_sem, gs_sem, gr_sem, es_sem, er_sem,
-        hs_sem, hr_sem, ns_sem, nr_sem,
+        hs_sem, hr_sem, ns_sem, nr_sem, solution, right_side, couple, partner, orient, owner_one, owner_two, in_sem,
     ) = more
     blocks, subs = sizes
     me = lax.axis_index("blk")
@@ -74,12 +74,27 @@
     planes = SUBLANES
     count_all = blocks * subs
     here = me * subs + sub
-
-    @pl.loop(1, count_all)
-    def _(step):
-        there = (here + step) % count_all
-        pl.semaphore_signal(pltpu.get_barrier_semaphore(), inc=1,
-                            device_id=(there // subs, there % subs), device_id_type=MESH)
+    fetch = [pltpu.make_async_copy(source, target, in_sem.at[n]) for n, (source, target) in enumerate(
+        ((solution_hbm, solution), (right_side_hbm, right_side), (couple_hbm, couple), (partner_hbm, partner),
+         (orient_hbm, orient), (owner_one_hbm, owner_one), (owner_two_hbm, owner_two)))]
+    for copy in fetch:
+        copy.start()
+
+    def after(index, step, length):
+        return jnp.where(index + step >= length, index + step - length, index + step)
+
+    def everyone(body):
+        for turn in range(subs):
+            part = after(sub, turn, subs)
+
+            @pl.loop(0 if turn else 1, blocks)
+            def _(step):
+                body(after(me, step, blocks), part)
+
+    everyone(lambda b, t: pl.semaphore_signal(
+        pltpu.get_barrier_semaphore(), inc=1, device_id=(b, t), device_id_type=MESH))
+    for copy in fetch[3:]:
+        copy.wait()
 
     def found(mapping, value):
         return lax.fori_loop(0, blocks, lambda n, best: jnp.where(mapping[n] == value, n, best), 0)
@@ -103,26 +118,34 @@
             return (0, last) + tuple(range(1, last))
         return (last,) if kind else (0,)
 
-    def send_edge(n, ref):
-        code = jnp.where(is_low, orient[down[me]], orient[me])
-        turned = permute(ref[...], lane ^ jnp.where(code // 2 == 1, BJ - 1, 0) ^ jnp.where(code % 2 == 1, LANES - BJ, 0))
-        swapped = jnp.concatenate([turned[:, r:r + 1] for r in range(rows - 1, -1, -1)], axis=1)
-        turned = jnp.where(code % 2 == 1, swapped, turned)
-
-        for kind, mine in ((1, is_low), (0, is_high)):
+    ends = ((1, is_low, 0, 0), (0, is_high, last, planes - 1))
+
+    def stage_edge(n, ref):
+        for kind, mine, own, at in ends:
             @pl.when(mine)
             def _():
-                edge = edge_a if kind else edge_w
-                at = 0 if kind else planes - 1
-                xsend[n] = turned[:, :, at:at + 1]
-                edge[n][me] = turned[:, :, at:at + 1]
-                own = 0 if kind else last
+                code = orient[down[me]] if kind else orient[me]
+                places = lane ^ jnp.where(code // 2 == 1, BJ - 1, 0) ^ jnp.where(code % 2 == 1, LANES - BJ, 0)
+                moved = permute(ref[...], places)
+                swapped = jnp.concatenate([moved[:, r:r + 1] for r in range(rows - 1, -1, -1)], axis=1)
+                moved = jnp.where(code % 2 == 1, swapped, moved)[:, :, at:at + 1]
+                xsend[n] = moved
+                (edge_a if kind else edge_w)[n][me] = moved
+
+    def each_edge(n, act):
+        for kind, mine, own, at in ends:
+            @pl.when(mine)
+            def _():
                 for t in targets(n, kind):
-                    first = 1 if t == own else 0
-
-                    @pl.loop(first, blocks)
+                    @pl.loop(1 if t == own else 0, blocks)
                     def _(step):
-                        edge_copy(n, (me + step) % blocks, t, kind, me).start()
+                        act(edge_copy(n, after(me, step, blocks), t, kind, me))
+
+    def start_edge(n):
+        each_edge(n, lambda copy: copy.start())
+
+    def finish_edge(n):
+        each_edge(n, lambda copy: copy.wait_send())
 
     def receive_edge(n):
         for kind in (0, 1):
@@ -136,7 +159,7 @@
                 def _():
                     @pl.loop(first, blocks)
                     def _(step):
-                        source = (me + step) % blocks
+                        source = after(me, step, blocks)
                         edge_copy(n, source, t, kind, source).wait_recv()
 
     def start_copy(source, target):
@@ -173,8 +196,6 @@
         @pl.loop(0, 6)
         def _(matrix):
             store[IM + matrix] = product(store[INV], store[RAW + 1 + matrix])
-
-    prepare(0, coef)
 
     def powers(base, second, sixteenth, count):
         coef[second] = product(coef[base], coef[base])
@@ -186,8 +207,6 @@
             run = product(jnp.where((count & bit) != 0, coef[index], identity), run)
         coef[second + 3] = run
 
-    powers(FWD, F2, F16, place + 1)
-    powers(BWD, B2, B16, planes - place)
 
     def combined():
         seventh = product(coef[B4], product(coef[B2], coef[BWD]))
@@ -232,11 +251,6 @@
             by *= 2
         return values
 
-    starts[sub] = solution[:, :, 0:1, :]
-    cg[...] = apply(INV, right_side[...])
-    upper = jnp.where(place == planes - 1, 0.0, pltpu.roll(solution[...], planes - 1, 2))
-    sf[...] = cg[...] + lateral(solution[...], IM) + apply(BWD, upper)
-
     def local(n):
         yf[...] = scan(sf[...], (FWD, F2, F4), False)
         tf[...] = cg[...] + lateral(yf[...], IM) + (yf[...] - sf[...])
@@ -250,25 +264,44 @@
             def _():
                 prefix_copy(n, sub, target).start()
 
-    local(0)
+    def finish_prefix(n):
+        for target in range(subs):
+            @pl.when(sub != target)
+            def _():
+                prefix_copy(n, sub, target).wait_send()
+
+    fetch[0].wait()
+    starts[sub] = solution[:, :, 0:1, :]
+    stage_edge(0, solution)
     pl.semaphore_wait(pltpu.get_barrier_semaphore(), count_all - 1)
-    send_edge(0, solution)
+    start_edge(0)
     for target in range(subs):
         @pl.when((sub > 0) & (sub != target))
         def _():
             start_copy(sub, target).start()
+    fetch[2].wait()
+    prepare(0, coef)
+    powers(FWD, F2, F16, place + 1)
+    powers(BWD, B2, B16, planes - place)
+    fetch[1].wait()
+    cg[...] = apply(INV, right_side[...])
+    upper = jnp.where(place == planes - 1, 0.0, pltpu.roll(solution[...], planes - 1, 2))
+    sf[...] = cg[...] + lateral(solution[...], IM) + apply(BWD, upper)
+    local(0)
     send_prefix(0)
     combined()
-    for number, store in ((1, coef_one), (2, coef_two)):
-        prepare(number, store)
-        width = BJ >> number
-        cells = rows * LANES >> (2 * number)
-        inside = lane < cells
-        masks = ((lane >= width) & inside, lane < cells - width,
-                 ((lane & (width - 1)) != 0) & inside, ((lane & (width - 1)) != width - 1) & inside)
-        for shift, mask in enumerate(masks):
-            for base in (RAW + 1, IM):
-                store[base + shift] = jnp.where(mask, store[base + shift], 0.0)
+
+    def prepare_coarse():
+        for number, store in ((1, coef_one), (2, coef_two)):
+            prepare(number, store)
+            width = BJ >> number
+            cells = rows * LANES >> (2 * number)
+            inside = lane < cells
+            masks = ((lane >= width) & inside, lane < cells - width,
+                     ((lane & (width - 1)) != 0) & inside, ((lane & (width - 1)) != width - 1) & inside)
+            for shift, mask in enumerate(masks):
+                for base in (RAW + 1, IM):
+                    store[base + shift] = jnp.where(mask, store[base + shift], 0.0)
 
     for n in range(SWEEPS_FINE):
         for source in range(subs):
@@ -311,10 +344,19 @@
         tf[...] = cg[...] + lateral(y, IM) + (y - (sf[...] + extra))
         zf[...] = scan(tf[...], (BWD, B2, B4), True) + apply(BP, wide[1, :, :, pl.ds(sub, 1), :])
         if n + 1 < SWEEPS_FINE:
-            send_edge(n + 1, zf)
+            stage_edge(n + 1, zf)
+            start_edge(n + 1)
             sf[...] = cg[...] + lateral(zf[...], IM) + (zf[...] - tf[...])
             local(n + 1)
             send_prefix(n + 1)
+            if n == 0:
+                prepare_coarse()
+                finish_edge(0)
+                finish_prefix(0)
+                for target in range(subs):
+                    @pl.when((sub > 0) & (sub != target))
+                    def _():
+                        start_copy(sub, target).wait_send()
 
     change = zf[...] - yf[...]
     lower = jnp.where(place == 0, -wide[0, :, :, pl.ds(sub, 1), :], pltpu.roll(change, 1, 2))
@@ -346,7 +388,7 @@
 
     @pl.loop(1, blocks)
     def _(step):
-        spread_copy(me, (me + step) % blocks).start()
+        spread_copy(me, after(me, step, blocks)).start()
 
     def across_copy(source, block, target):
         return pltpu.make_async_remote_copy(
@@ -355,22 +397,10 @@
             device_id=(me, target), device_id_type=MESH)
 
     for step in range(1, subs):
-        across_copy(sub, me, (sub + step) % subs).start()
-
-    @pl.loop(1, blocks)
-    def _(step):
-        source = (me + step) % blocks
-        spread_copy(source, source).wait_recv()
-        for turn in range(1, subs):
-            across_copy(sub, source, (sub + turn) % subs).start()
-
-    @pl.loop(0, blocks)
-    def _(block):
-        for turn in range(1, subs):
-            source = (sub + turn) % subs
-            across_copy(source, block, source).wait_recv()
-
-    send_edge(SWEEPS_FINE, zf)
+        across_copy(sub, me, after(sub, step, subs)).start()
+
+    stage_edge(SWEEPS_FINE, zf)
+    start_edge(SWEEPS_FINE)
     low_recv[0] = zf[:, :, planes - 1:planes, :]
 
     def halo_copy(target):
@@ -381,6 +411,53 @@
     @pl.when(jnp.logical_not(is_high))
     def _():
         halo_copy(sub + 1).start()
+
+    @pl.loop(1, blocks)
+    def _(step):
+        source = after(me, step, blocks)
+        spread_copy(source, source).wait_recv()
+        for turn in range(1, subs):
+            across_copy(sub, source, after(sub, turn, subs)).start()
+
+    for n in range(1, SWEEPS_FINE):
+        finish_edge(n)
+        finish_prefix(n)
+
+    @pl.loop(1, blocks)
+    def _(step):
+        spread_copy(me, after(me, step, blocks)).wait_send()
+
+    receive_edge(SWEEPS_FINE)
+
+    @pl.when(is_low)
+    def _():
+        low_recv[1] = edge_w[SWEEPS_FINE][down[me]]
+
+    @pl.when(is_high)
+    def _():
+        fresh = apply(RAW + 6, edge_a[SWEEPS_FINE][partner[me]], 1)
+        sf[:, :, planes - 1:planes, :] = sf[:, :, planes - 1:planes, :] + fresh
+
+    @pl.when(jnp.logical_not(is_low))
+    def _():
+        halo_copy(sub).wait_recv()
+
+    sf[:, :, 0:1, :] = sf[:, :, 0:1, :] + apply(RAW + 5, low_recv[1], 1)
+    residual = sf[...]
+    squares_recv[here] = jnp.sum((residual * residual).reshape(NV * rows * SUBLANES, LANES), axis=0, keepdims=True)
+
+    def norm_copy(source, b, t):
+        return pltpu.make_async_remote_copy(
+            src_ref=squares_recv.at[source], dst_ref=squares_recv.at[source], send_sem=ns_sem.at[b * subs + t],
+            recv_sem=nr_sem.at[source], device_id=(b, t), device_id_type=MESH)
+
+    everyone(lambda b, t: norm_copy(here, b, t).start())
+
+    @pl.loop(0, blocks)
+    def _(block):
+        for turn in range(1, subs):
+            source = after(sub, turn, subs)
+            across_copy(source, block, source).wait_recv()
 
     def use(store, index, values):
         cut = values.reshape(NV, -1, SUBLANES, LANES)
@@ -517,34 +594,6 @@
     depth_one = field_f.shape[1]
     total = level(coef_one, cells_one, BJ // 2, field_f, field_c, field_p, field_v, field_y, SWEEPS_MID)
     norms[1:2, :] = jnp.broadcast_to(root_mean(total, size // 8), (1, LANES))
-
-    receive_edge(SWEEPS_FINE)
-
-    @pl.when(is_low)
-    def _():
-        low_recv[1] = edge_w[SWEEPS_FINE][down[me]]
-
-    @pl.when(is_high)
-    def _():
-        fresh = apply(RAW + 6, edge_a[SWEEPS_FINE][partner[me]], 1)
-        sf[:, :, planes - 1:planes, :] = sf[:, :, planes - 1:planes, :] + fresh
-
-    @pl.when(jnp.logical_not(is_low))
-    def _():
-        halo_copy(sub).wait_recv()
-
-    sf[:, :, 0:1, :] = sf[:, :, 0:1, :] + apply(RAW + 5, low_recv[1], 1)
-    residual = sf[...]
-    squares_recv[here] = jnp.sum((residual * residual).reshape(NV * rows * SUBLANES, LANES), axis=0, keepdims=True)
-
-    def norm_copy(source, target):
-        return pltpu.make_async_remote_copy(
-            src_ref=squares_recv.at[source], dst_ref=squares_recv.at[source], send_sem=ns_sem.at[target],
-            recv_sem=nr_sem.at[source], device_id=(target // subs, target % subs), device_id_type=MESH)
-
-    @pl.loop(1, count_all)
-    def _(step):
-        norm_copy(here, (here + step) % count_all).start()
 
     s_row = lax.broadcasted_iota(jnp.int32, (LANES, LANES), 0)
     s_col = lax.broadcasted_iota(jnp.int32, (LANES, LANES), 1)
@@ -582,52 +631,21 @@
         grow = ((((s_col + r * LANES) >> 5) * half) + ((s_col & (BJ - 1)) >> 1) == s_row).astype(jnp.float32)
         corrected[:, r] = zf[:, r] + chosen(spread[...], grow).reshape(NV, SUBLANES, LANES)
 
-    @pl.loop(1, count_all)
-    def _(step):
-        source = (here + step) % count_all
-        norm_copy(source, source).wait_recv()
-
-    total = jnp.sum(squares_recv[...].reshape(count_all, LANES), axis=0, keepdims=True)
-    norms[0:1, :] = jnp.broadcast_to(root_mean(total, size), (1, LANES))
-
-    for n in range(SWEEPS_FINE + 1):
-        for kind, mine in ((1, is_low), (0, is_high)):
-            @pl.when(mine)
-            def _():
-                own = 0 if kind else last
-                for t in targets(n, kind):
-                    first = 1 if t == own else 0
-
-                    @pl.loop(first, blocks)
-                    def _(step):
-                        edge_copy(n, (me + step) % blocks, t, kind, me).wait_send()
-
-    for target in range(subs):
-        @pl.when((sub > 0) & (sub != target))
-        def _():
-            start_copy(sub, target).wait_send()
-
-        @pl.when(sub != target)
-        def _():
-            for n in range(SWEEPS_FINE):
-                prefix_copy(n, sub, target).wait_send()
+    @pl.loop(0, blocks)
+    def _(block):
+        for turn in range(1, subs):
+            across_copy(sub, block, after(sub, turn, subs)).wait_send()
+
+    finish_edge(SWEEPS_FINE)
 
     @pl.when(jnp.logical_not(is_high))
     def _():
         halo_copy(sub + 1).wait_send()
 
-    @pl.loop(1, blocks)
-    def _(step):
-        spread_copy(me, (me + step) % blocks).wait_send()
-
-    @pl.loop(0, blocks)
-    def _(block):
-        for turn in range(1, subs):
-            across_copy(sub, block, (sub + turn) % subs).wait_send()
-
-    @pl.loop(1, count_all)
-    def _(step):
-        norm_copy(here, (here + step) % count_all).wait_send()
+    everyone(lambda b, t: norm_copy(b * subs + t, b, t).wait_recv())
+    total = jnp.sum(squares_recv[...].reshape(count_all, LANES), axis=0, keepdims=True)
+    norms[0:1, :] = jnp.broadcast_to(root_mean(total, size), (1, LANES))
+    everyone(lambda b, t: norm_copy(here, b, t).wait_send())
 
 
 def finish(corrected, one, two, norms, out, out_one, out_two, out_norms):
@@ -651,6 +669,7 @@
 
     vmem = pl.BlockSpec(memory_space=pltpu.VMEM)
     smem = pl.BlockSpec(memory_space=pltpu.SMEM)
+    hbm = pl.BlockSpec(memory_space=pl.ANY)
     f32 = jnp.float32
     fine = pltpu.VMEM((NV, rows, planes, LANES), f32)
     plane = (NV, rows, 1, LANES)
@@ -661,6 +680,7 @@
     dma = pltpu.SemaphoreType.DMA
     edges = SWEEPS_FINE + 1
     everyone = blocks * subs
+    couple = couple.transpose(2, 3, 0, 1)
     results = pl.pallas_call(
         functools.partial(kernel, (blocks, subs)),
         name="vcycle",
@@ -670,7 +690,7 @@
             pltpu.VMEM((NV, planes // 4, LANES), f32),
             pltpu.VMEM((3, LANES), f32),
         ),
-        in_specs=[vmem, vmem, smem, smem, smem, smem, smem],
+        in_specs=[hbm] * 7,
         out_specs=(vmem, vmem, vmem, vmem),
         scratch_shapes=[
             pltpu.VMEM((29,) + matrix, f32), pltpu.VMEM((14,) + matrix, f32), pltpu.VMEM((14,) + matrix, f32),
@@ -691,9 +711,10 @@
             dma((SWEEPS_FINE, subs)), dma((SWEEPS_FINE, subs)),
             dma((blocks,)), dma((blocks,)), dma((subs, blocks)), dma((subs, blocks)),
             dma((1,)), dma((1,)), dma((everyone,)), dma((everyone,)),
+            fine, fine, pltpu.SMEM(couple.shape, f32), *[pltpu.SMEM((blocks,), jnp.int32)] * 4, dma((7,)),
         ],
         compiler_params=pltpu.CompilerParams(collective_id=0, has_side_effects=True, vmem_limit_bytes=60 * 1024 * 1024),
-    )(tiled(solution), tiled(right_side), couple.transpose(2, 3, 0, 1), partner, orient, owner_one, owner_two)
+    )(tiled(solution), tiled(right_side), couple, partner, orient, owner_one, owner_two)
     return pl.pallas_call(
         finish,
         name="finish",

time: 47.7 us -> 40.4 us (0.85)
  Pallas kernels: 46.8 us -> 39.1 us
    pallas_call x1, Pallas kernels: 46.2 us -> 38.5 us  [shards(): pl.pallas_call(functools.partial(kernel, (blocks, subs)), name='vcycle',...]
where the time goes in v3:
time: 40.4 us; the launch traced here: 39.8 us
  Pallas kernels  39.1 us (97%)
  between operations  0.64 us (2%)
    pallas_call x1, Pallas kernels, shards(): pl.pallas_call(functools.partial(kernel, (blocks, subs)), name='vcycle',...  38.5 us

profile of v3, /device:TPU:0, one launch (start us, length us, event | category | flops | bytes accessed | tf_op | source)
XLA Modules:
  0.0 39.8 jit_solution(8751740163262216916)
XLA Ops:
  0.6 38.5 %vcycle.1 = (f32[5,4,8,128]{3,2,1,0:T(8,128)S(1)}, f32[5,4,128]{2,1,0:T(4,128)S(1)}, f32[5,2,128]{2,1,0:T(2,128)S(1)}, f32[3,128]{1,0:T(4,128)S(1)}) custom-call(f32[5,4,8,128]{3,2,1,0:T(8,128)} %bitcast.7, f32[5,4,8,128]{3,2,1,0:T(8,128)} %bitcast.8, f32[5,5,3,7]{3,2,1,0:T(4,128)} %bitcast.9, s32[8]{0:T(128)} %partner_hbm.1, s32[8]{0:T(128)} %orient_hbm.1, ...), custom_call_target="tpu_custom_call" | custom-call | tf_op jit(solution)/shard_map/vcycle/pallas_call | solution.py:684
  39.1 0.7 %finish.1 = (f32[5,1,8,512]{3,2,1,0:T(8,128)}, f32[5,1,4,128]{3,2,1,0:T(4,128)}, f32[5,1,2,32]{3,2,1,0:T(2,128)}, f32[3]{0:T(128)}) custom-call(f32[5,4,8,128]{3,2,1,0:T(8,128)S(1)} %get-tuple-element.8.corrected, f32[5,4,128]{2,1,0:T(4,128)S(1)} %get-tuple-element.9.one, f32[5,2,128]{2,1,0:T(2,128)S(1)} %get-tuple-element.10.two, ...), custom_call_target="tpu_custom_call" | custom-call | tf_op jit(solution)/shard_map/finish/pallas_call | solution.py:718

commit v4 on v3

--- a/solution.py
+++ b/solution.py
@@ -63,6 +63,7 @@
         two_f, two_c, two_p, two_v, two_y, spread,
         xs_sem, xw_sem, xa_sem, us_sem, ur_sem, ps_sem, pr_sem, gs_sem, gr_sem, es_sem, er_sem,
         hs_sem, hr_sem, ns_sem, nr_sem, solution, right_side, couple, partner, orient, owner_one, owner_two, in_sem,
+        totals, ts_sem, tr_sem,
     ) = more
     blocks, subs = sizes
     me = lax.axis_index("blk")
@@ -83,6 +84,9 @@
     def after(index, step, length):
         return jnp.where(index + step >= length, index + step - length, index + step)
 
+    def peer(step):
+        return after(me, step, blocks)
+
     def everyone(body):
         for turn in range(subs):
             part = after(sub, turn, subs)
@@ -97,13 +101,10 @@
         copy.wait()
 
     def found(mapping, value):
-        return lax.fori_loop(0, blocks, lambda n, best: jnp.where(mapping[n] == value, n, best), 0)
-
-    @pl.loop(0, blocks)
-    def _(n):
-        down[n] = found(partner, n)
-
-    held = (found(owner_one, me), found(owner_two, me))
+        return lax.fori_loop(0, blocks, lambda n, best: jnp.where(mapping[n] == value, n, best), 0,
+                             unroll=blocks <= SUBLANES)
+
+    source_below = found(partner, me)
     lane = lax.broadcasted_iota(jnp.int32, (1, LANES), 1)
     place = lax.broadcasted_iota(jnp.int32, (SUBLANES, LANES), 0)
 
@@ -124,7 +125,7 @@
         for kind, mine, own, at in ends:
             @pl.when(mine)
             def _():
-                code = orient[down[me]] if kind else orient[me]
+                code = orient[source_below] if kind else orient[me]
                 places = lane ^ jnp.where(code // 2 == 1, BJ - 1, 0) ^ jnp.where(code % 2 == 1, LANES - BJ, 0)
                 moved = permute(ref[...], places)
                 swapped = jnp.concatenate([moved[:, r:r + 1] for r in range(rows - 1, -1, -1)], axis=1)
@@ -139,7 +140,7 @@
                 for t in targets(n, kind):
                     @pl.loop(1 if t == own else 0, blocks)
                     def _(step):
-                        act(edge_copy(n, after(me, step, blocks), t, kind, me))
+                        act(edge_copy(n, peer(step), t, kind, me))
 
     def start_edge(n):
         each_edge(n, lambda copy: copy.start())
@@ -303,6 +304,12 @@
                 for base in (RAW + 1, IM):
                     store[base + shift] = jnp.where(mask, store[base + shift], 0.0)
 
+    @pl.loop(0, blocks)
+    def _(n):
+        down[n] = found(partner, n)
+
+    held = (found(owner_one, me), found(owner_two, me))
+
     for n in range(SWEEPS_FINE):
         for source in range(subs):
             @pl.when(sub != source)
@@ -311,7 +318,7 @@
                     start_copy(source, sub).wait_recv()
                 prefix_copy(n, source, sub).wait_recv()
         receive_edge(n)
-        below = edge_w[n][down[me]]
+        below = edge_w[n][source_below]
         above = edge_a[n][partner[me]]
         missing = above if n == 0 else above - old_above[...]
         ahead = jnp.where(place == subs + last, missing, 0.0)
@@ -376,10 +383,8 @@
     count = NV * planes // 2
     rsum[...] = reduced * 0.125
     gathered[sub, me, 0:count, :] = rsum[pl.ds(0, count, stride=2), :] + rsum[pl.ds(1, count, stride=2), :]
-    tail = gathered.shape[2] - count - 2 * NV
     gathered[sub, me, count:count + NV, :] = rsum[pl.ds(NV * planes + planes - 1, NV, stride=planes), :]
     gathered[sub, me, count + NV:count + 2 * NV, :] = rsum[pl.ds(NV * planes, NV, stride=planes), :]
-    gathered[sub, me, count + 2 * NV:, :] = jnp.zeros((tail, LANES), jnp.float32)
 
     def spread_copy(source, target):
         return pltpu.make_async_remote_copy(
@@ -388,7 +393,7 @@
 
     @pl.loop(1, blocks)
     def _(step):
-        spread_copy(me, after(me, step, blocks)).start()
+        spread_copy(me, peer(step)).start()
 
     def across_copy(source, block, target):
         return pltpu.make_async_remote_copy(
@@ -431,7 +436,7 @@
 
     @pl.when(is_low)
     def _():
-        low_recv[1] = edge_w[SWEEPS_FINE][down[me]]
+        low_recv[1] = edge_w[SWEEPS_FINE][source_below]
 
     @pl.when(is_high)
     def _():
@@ -444,14 +449,21 @@
 
     sf[:, :, 0:1, :] = sf[:, :, 0:1, :] + apply(RAW + 5, low_recv[1], 1)
     residual = sf[...]
-    squares_recv[here] = jnp.sum((residual * residual).reshape(NV * rows * SUBLANES, LANES), axis=0, keepdims=True)
-
-    def norm_copy(source, b, t):
+    squares_recv[me] = jnp.sum((residual * residual).reshape(NV * rows * SUBLANES, LANES), axis=0, keepdims=True)
+
+    def norm_copy(source, target):
         return pltpu.make_async_remote_copy(
-            src_ref=squares_recv.at[source], dst_ref=squares_recv.at[source], send_sem=ns_sem.at[b * subs + t],
-            recv_sem=nr_sem.at[source], device_id=(b, t), device_id_type=MESH)
-
-    everyone(lambda b, t: norm_copy(here, b, t).start())
+            src_ref=squares_recv.at[source], dst_ref=squares_recv.at[source], send_sem=ns_sem.at[target],
+            recv_sem=nr_sem.at[source], device_id=(target, sub), device_id_type=MESH)
+
+    def total_copy(source, target):
+        return pltpu.make_async_remote_copy(
+            src_ref=totals.at[source], dst_ref=totals.at[source], send_sem=ts_sem.at[target],
+            recv_sem=tr_sem.at[source], device_id=(me, target), device_id_type=MESH)
+
+    @pl.loop(1, blocks)
+    def _(step):
+        norm_copy(me, peer(step)).start()
 
     @pl.loop(0, blocks)
     def _(block):
@@ -594,6 +606,19 @@
     depth_one = field_f.shape[1]
     total = level(coef_one, cells_one, BJ // 2, field_f, field_c, field_p, field_v, field_y, SWEEPS_MID)
     norms[1:2, :] = jnp.broadcast_to(root_mean(total, size // 8), (1, LANES))
+
+    @pl.loop(1, blocks)
+    def _(step):
+        source = peer(step)
+        norm_copy(source, source).wait_recv()
+
+    totals[sub] = jnp.sum(squares_recv[...].reshape(blocks, LANES), axis=0, keepdims=True)
+    for turn in range(1, subs):
+        total_copy(sub, after(sub, turn, subs)).start()
+
+    @pl.loop(1, blocks)
+    def _(step):
+        norm_copy(me, peer(step)).wait_send()
 
     s_row = lax.broadcasted_iota(jnp.int32, (LANES, LANES), 0)
     s_col = lax.broadcasted_iota(jnp.int32, (LANES, LANES), 1)
@@ -642,10 +667,13 @@
     def _():
         halo_copy(sub + 1).wait_send()
 
-    everyone(lambda b, t: norm_copy(b * subs + t, b, t).wait_recv())
-    total = jnp.sum(squares_recv[...].reshape(count_all, LANES), axis=0, keepdims=True)
+    for turn in range(1, subs):
+        source = after(sub, turn, subs)
+        total_copy(source, source).wait_recv()
+    total = jnp.sum(totals[...].reshape(subs, LANES), axis=0, keepdims=True)
     norms[0:1, :] = jnp.broadcast_to(root_mean(total, size), (1, LANES))
-    everyone(lambda b, t: norm_copy(here, b, t).wait_send())
+    for turn in range(1, subs):
+        total_copy(sub, after(sub, turn, subs)).wait_send()
 
 
 def finish(corrected, one, two, norms, out, out_one, out_two, out_norms):
@@ -676,10 +704,9 @@
     mid = pltpu.VMEM((NV, tall // 2, blocks, LANES), f32)
     low = pltpu.VMEM((NV, tall // 4, blocks, LANES), f32)
     matrix = (NV, NV, SUBLANES, LANES)
-    payload = -(-(NV * planes // 2 + 2 * NV) // SUBLANES) * SUBLANES
+    payload = NV * planes // 2 + 2 * NV
     dma = pltpu.SemaphoreType.DMA
     edges = SWEEPS_FINE + 1
-    everyone = blocks * subs
     couple = couple.transpose(2, 3, 0, 1)
     results = pl.pallas_call(
         functools.partial(kernel, (blocks, subs)),
@@ -702,7 +729,7 @@
             pltpu.VMEM((subs, blocks, payload, LANES), f32),
             pltpu.VMEM((2 * NV * planes, LANES), f32),
             pltpu.VMEM((2,) + plane, f32),
-            pltpu.VMEM((everyone, 1, LANES), f32),
+            pltpu.VMEM((blocks, 1, LANES), f32),
             pltpu.SMEM((blocks,), jnp.int32),
             mid, mid, mid, mid, mid, low, low, low, low, low,
             pltpu.VMEM((NV * planes, LANES), f32),
@@ -710,8 +737,9 @@
             dma((subs,)), dma((subs,)),
             dma((SWEEPS_FINE, subs)), dma((SWEEPS_FINE, subs)),
             dma((blocks,)), dma((blocks,)), dma((subs, blocks)), dma((subs, blocks)),
-            dma((1,)), dma((1,)), dma((everyone,)), dma((everyone,)),
+            dma((1,)), dma((1,)), dma((blocks,)), dma((blocks,)),
             fine, fine, pltpu.SMEM(couple.shape, f32), *[pltpu.SMEM((blocks,), jnp.int32)] * 4, dma((7,)),
+            pltpu.VMEM((subs, 1, LANES), f32), dma((subs,)), dma((subs,)),
         ],
         compiler_params=pltpu.CompilerParams(collective_id=0, has_side_effects=True, vmem_limit_bytes=60 * 1024 * 1024),
     )(tiled(solution), tiled(right_side), couple, partner, orient, owner_one, owner_two)

time: 40.4 us -> 38.8 us (0.960)
  Pallas kernels: 39.1 us -> 37.9 us
    pallas_call x1, Pallas kernels: 38.5 us -> 37.3 us  [shards(): pl.pallas_call(functools.partial(kernel, (blocks, subs)), name='vcycle',...]
where the time goes in v4:
time: 38.8 us; the launch traced here: 38.6 us
  Pallas kernels  37.9 us (98%)
  between operations  0.64 us (2%)
    pallas_call x1, Pallas kernels, shards(): pl.pallas_call(functools.partial(kernel, (blocks, subs)), name='vcycle',...  37.3 us

profile of v4, /device:TPU:0, one launch (start us, length us, event | category | flops | bytes accessed | tf_op | source)
XLA Modules:
  0.0 38.6 jit_solution(12649381033370526665)
XLA Ops:
  0.6 37.3 %vcycle.1 = (f32[5,4,8,128]{3,2,1,0:T(8,128)S(1)}, f32[5,4,128]{2,1,0:T(4,128)S(1)}, f32[5,2,128]{2,1,0:T(2,128)S(1)}, f32[3,128]{1,0:T(4,128)S(1)}) custom-call(f32[5,4,8,128]{3,2,1,0:T(8,128)} %bitcast.7, f32[5,4,8,128]{3,2,1,0:T(8,128)} %bitcast.8, f32[5,5,3,7]{3,2,1,0:T(4,128)} %bitcast.9, s32[8]{0:T(128)} %partner_hbm.1, s32[8]{0:T(128)} %orient_hbm.1, ...), custom_call_target="tpu_custom_call" | custom-call | tf_op jit(solution)/shard_map/vcycle/pallas_call | solution.py:711
  37.9 0.7 %finish.1 = (f32[5,1,8,512]{3,2,1,0:T(8,128)}, f32[5,1,4,128]{3,2,1,0:T(4,128)}, f32[5,1,2,32]{3,2,1,0:T(2,128)}, f32[3]{0:T(128)}) custom-call(f32[5,4,8,128]{3,2,1,0:T(8,128)S(1)} %get-tuple-element.8.corrected, f32[5,4,128]{2,1,0:T(4,128)S(1)} %get-tuple-element.9.one, f32[5,2,128]{2,1,0:T(2,128)S(1)} %get-tuple-element.10.two, ...), custom_call_target="tpu_custom_call" | custom-call | tf_op jit(solution)/shard_map/finish/pallas_call | solution.py:746

commit v5 on v4

--- a/solution.py
+++ b/solution.py
@@ -521,7 +521,7 @@
 
     def level(store, cells, width, g, c, p, v, y, sweeps):
         depth = g.shape[1]
-        chunk = max(1, 4 * SUBLANES // blocks)
+        chunk = max(1, 2 * SUBLANES // blocks)
         steps = depth // chunk
 
         def repeat(body, start, number):

time: 38.8 us -> 38.7 us (level)
  no operation moved by 1% of the time
where the time goes in v5:
time: 38.7 us; the launch traced here: 38.5 us
  Pallas kernels  37.8 us (98%)
  between operations  0.64 us (2%)
    pallas_call x1, Pallas kernels, shards(): pl.pallas_call(functools.partial(kernel, (blocks, subs)), name='vcycle',...  37.2 us

profile of v5, /device:TPU:0, one launch (start us, length us, event | category | flops | bytes accessed | tf_op | source)
XLA Modules:
  0.0 38.5 jit_solution(3712983918924004464)
XLA Ops:
  0.6 37.2 %vcycle.1 = (f32[5,4,8,128]{3,2,1,0:T(8,128)S(1)}, f32[5,4,128]{2,1,0:T(4,128)S(1)}, f32[5,2,128]{2,1,0:T(2,128)S(1)}, f32[3,128]{1,0:T(4,128)S(1)}) custom-call(f32[5,4,8,128]{3,2,1,0:T(8,128)} %bitcast.7, f32[5,4,8,128]{3,2,1,0:T(8,128)} %bitcast.8, f32[5,5,3,7]{3,2,1,0:T(4,128)} %bitcast.9, s32[8]{0:T(128)} %partner_hbm.1, s32[8]{0:T(128)} %orient_hbm.1, ...), custom_call_target="tpu_custom_call" | custom-call | tf_op jit(solution)/shard_map/vcycle/pallas_call | solution.py:711
  37.8 0.7 %finish.1 = (f32[5,1,8,512]{3,2,1,0:T(8,128)}, f32[5,1,4,128]{3,2,1,0:T(4,128)}, f32[5,1,2,32]{3,2,1,0:T(2,128)}, f32[3]{0:T(128)}) custom-call(f32[5,4,8,128]{3,2,1,0:T(8,128)S(1)} %get-tuple-element.8.corrected, f32[5,4,128]{2,1,0:T(4,128)S(1)} %get-tuple-element.9.one, f32[5,2,128]{2,1,0:T(2,128)S(1)} %get-tuple-element.10.two, ...), custom_call_target="tpu_custom_call" | custom-call | tf_op jit(solution)/shard_map/finish/pallas_call | solution.py:746
